TPU v7x, 32 devices: a whole 2x2x4 slice. The times are simulated.
32 devices in a mesh: gx: 8 (over z, x), col: 4 (over y, core).
Axes of the slice: x: 2, y: 2, z: 4, core: 2. Of those that a mesh axis runs over, the one named last changes fastest.
Arguments:
- grid_field: bfloat16 [64, 32, 256, 128], P('col', 'gx'), may hold values from -6 to 6
- tucker_core: float32 [2, 32, 32, 8, 8, 4], P(None, 'col'), may hold values from -0.5 to 0.5
- in_factor: float32 [64, 32], P('col'), may hold values from -0.75 to 0.75
- out_factor: float32 [64, 32], P('col'), may hold values from -1 to 1
- x_factor: float32 [32, 8], replicated, may hold values from -4 to 4
- y_factor: float32 [32, 8], replicated, may hold values from -4 to 4
- z_factor: float32 [16, 4], replicated, may hold values from -4 to 4
- kx_reach: int32 [32, 16], replicated, may hold values from 1 to 17
Outputs:
- spectral_out: bfloat16 [64, 32, 256, 128], P('col', 'gx')
All inputs are finite; a program needn't handle non-finite values.
Results may differ from a plain program's by a relative error of at most 0.001.
Values sent between devices are 32-bit elements; how exact they have to be, the bound alone decides.
A program may use at most 64 MiB of HBM per device.

v0:
```python
import math

import jax
import jax.numpy as jnp
from jax import lax
from jax.sharding import PartitionSpec as P


def slot_freq(slot_count):
    slot_index = jnp.arange(slot_count, dtype=jnp.int32)
    return jnp.where(slot_index < slot_count // 2, slot_index, slot_index - slot_count)


def phase_table(positions, extent, slot_count, direction):
    phase_steps = positions[:, None] * slot_freq(slot_count)[None, :] % extent
    radians = 2.0 * math.pi / extent * phase_steps.astype(jnp.float32)
    norm_scale = 1.0 / math.sqrt(extent)
    cosine = jnp.cos(radians) * norm_scale
    sine_part = direction * jnp.sin(radians) * norm_scale
    return jnp.stack([jnp.stack([cosine, -sine_part], 1), jnp.stack([sine_part, cosine], 1)], 1)


def z_tables(grid_z, modes_z):
    z_index = jnp.arange(grid_z, dtype=jnp.int32)
    kz_index = jnp.arange(modes_z, dtype=jnp.int32)
    phase_steps = z_index[:, None] * kz_index[None, :] % grid_z
    radians = 2.0 * math.pi / grid_z * phase_steps.astype(jnp.float32)
    norm_scale = 1.0 / math.sqrt(grid_z)
    cosine = jnp.cos(radians) * norm_scale
    sine_part = jnp.sin(radians) * norm_scale
    forward = jnp.stack([cosine, -sine_part], 1)
    weight = jnp.where(kz_index == 0, 1.0, 2.0).astype(jnp.float32)
    backward = jnp.stack([(cosine * weight[None, :]).T, -(sine_part * weight[None, :]).T], 0)
    return (forward, backward)


def per_device(
    grid_field, tucker_core, in_factor, out_factor, x_factor, y_factor, z_factor, kx_reach
):
    highest = lax.Precision.HIGHEST
    channels, planes, grid_y, grid_z = grid_field.shape
    modes_x = x_factor.shape[0]
    modes_y = y_factor.shape[0]
    modes_z = z_factor.shape[0]
    width_gx = lax.axis_size("gx")
    grid_x = planes * width_gx
    columns = modes_y * modes_z
    col_dev = columns // width_gx
    slab_index = lax.axis_index("gx")
    z_forward, z_backward = z_tables(grid_z, modes_z)
    y_forward = phase_table(jnp.arange(grid_y, dtype=jnp.int32), grid_y, modes_y, 1.0)
    x_forward = phase_table(jnp.arange(grid_x, dtype=jnp.int32), grid_x, modes_x, 1.0)
    values = grid_field.astype(jnp.float32)
    z_spectrum = jnp.einsum("cxyz,zpl->cxply", values, z_forward, precision=highest)
    y_spectrum = jnp.einsum("cxply,ypqj->qcxjl", z_spectrum, y_forward, precision=highest)
    y_spectrum = y_spectrum.reshape(2, channels, planes, columns)
    first_col = slab_index * col_dev
    reach_dev = lax.dynamic_slice_in_dim(kx_reach.reshape(-1), first_col, col_dev)
    kept_mask = (jnp.abs(slot_freq(modes_x))[:, None] < reach_dev[None, :]).astype(jnp.float32)
    arrived = lax.all_to_all(y_spectrum, "gx", split_axis=3, concat_axis=2, tiled=True)
    spectrum = jnp.einsum("pcxm,xpqk->qckm", arrived, x_forward, precision=highest)
    partial_value = jnp.einsum("qckm,cr->qrkm", spectrum, in_factor, precision=highest)
    amplitude = lax.psum_scatter(partial_value, "col", scatter_dimension=1, tiled=True)
    amplitude = amplitude * kept_mask[None, None]
    column = first_col + jnp.arange(col_dev, dtype=jnp.int32)
    pick_y = (column[:, None] // modes_z == jnp.arange(modes_y, dtype=jnp.int32)[None, :]).astype(
        jnp.float32
    )
    pick_z = (column[:, None] % modes_z == jnp.arange(modes_z, dtype=jnp.int32)[None, :]).astype(
        jnp.float32
    )
    y_rows = jnp.dot(pick_y, y_factor, precision=highest)
    z_rows = jnp.dot(pick_z, z_factor, precision=highest)
    core_cols = jnp.einsum("prsabe,mb,me->prsam", tucker_core, y_rows, z_rows, precision=highest)
    kernel = jnp.einsum("prsam,ka->prskm", core_cols, x_factor, precision=highest)
    mixed_re = jnp.einsum("rskm,rkm->skm", kernel[0], amplitude[0], precision=highest) - jnp.einsum(
        "rskm,rkm->skm", kernel[1], amplitude[1], precision=highest
    )
    mixed_im = jnp.einsum("rskm,rkm->skm", kernel[0], amplitude[1], precision=highest) + jnp.einsum(
        "rskm,rkm->skm", kernel[1], amplitude[0], precision=highest
    )
    mixed_sum = lax.psum(jnp.stack([mixed_re, mixed_im]), "col")
    out_spec = jnp.einsum("os,qskm->qokm", out_factor, mixed_sum, precision=highest)
    x_backward = phase_table(jnp.arange(grid_x, dtype=jnp.int32), grid_x, modes_x, -1.0)
    x_values = jnp.einsum("pckm,xpqk->qcxm", out_spec, x_backward, precision=highest)
    returned = lax.all_to_all(x_values, "gx", split_axis=2, concat_axis=3, tiled=True)
    returned = returned.reshape(2, channels, planes, modes_y, modes_z)
    y_backward = phase_table(jnp.arange(grid_y, dtype=jnp.int32), grid_y, modes_y, -1.0)
    y_values = jnp.einsum("pcxjl,ypqj->cxqly", returned, y_backward, precision=highest)
    result = jnp.einsum("cxqly,qlz->cxyz", y_values, z_backward, precision=highest)
    return result.astype(jnp.bfloat16)


def solution(mesh):
    return jax.shard_map(
        per_device,
        mesh=mesh,
        in_specs=(
            P("col", "gx", None, None),
            P(None, "col", None, None, None, None),
            P("col", None),
            P("col", None),
            P(),
            P(),
            P(),
            P(),
        ),
        out_specs=P("col", "gx", None, None),
        check_vma=False,
    )
```

profile of v0, /device:TPU:0, one launch (start us, length us, event | category | flops | bytes accessed | tf_op | source)
XLA Modules:
  0.0 163.9 jit_solution(2289638814313260271)
XLA Ops:
  6.5 0.1 multiply_negate_fusion.1
  6.6 0.2 fusion.58
  6.8 6.5 %fusion = f32[2,16,16,4,256]{4,1,0,3,2:T(8,128)S(1)} fusion(bf16[16,4,256,128]{3,2,1,0:T(8,128)(2,1)} %param.8, f32[128,1,16]{0,2,1:T(8,128)S(1)} %get-tuple-element.35, f32[128,1,16]{0,2,1:T(8,128)S(1)} %get-tuple-element.36), kind=kOutput, calls=%fused_computation.3 | convolution fusion | flops 805310464 | bytes 6307840 | tf_op jit(solution)/shard_map/cxyz,zpl->cxply/dot_general | solution.py:54
  13.4 1.8 %fusion.9 = f32[2,16,4,32,16]{3,4,2,1,0:T(8,128)S(1)} fusion(f32[2,16,16,4,256]{4,1,0,3,2:T(8,128)S(1)} %fusion, f32[256,1,2,32]{0,3,1,2:T(8,128)S(1)} %get-tuple-element.14, f32[256,1,2,32]{0,3,1,2:T(8,128)S(1)} %get-tuple-element.15), kind=kOutput, calls=%fused_computation.19 | convolution fusion | flops 402685952 | bytes 2490368 | tf_op jit(solution)/shard_map/cxply,ypqj->qcxjl/dot_general | solution.py:55
  15.2 2.7 %copy.101 = f32[2,16,4,32,16]{1,2,0,4,3:T(4,128)} copy(f32[2,16,4,32,16]{3,4,2,1,0:T(8,128)S(1)} %fusion.9) | data formatting | bytes 524288 | tf_op jit(solution)/shard_map/reshape | solution.py:56
  17.9 3.8 %reshape.675 = f32[8,1,8192]{2,1,0:T(1,128)} reshape(f32[512,2,4,16]{3,2,1,0:T(4,128)} %bitcast.192) | data formatting | bytes 524288
  21.6 7.3 %all-to-all-start = ((f32[8,1,8192]{2,1,0:T(1,128)}), f32[8,1,8192]{2,1,0:T(1,128)S(1)}, u32[]{:S(2)}, u32[]{:S(2)}) async-start(f32[8,1,8192]{2,1,0:T(1,128)} %reshape.675), calls=%async_computation | async-start | bytes 524288 | tf_op jit(solution)/shard_map/all_to_all | solution.py:60
  28.9 0.0 reduce-scatter.2.cloned.1.call-start
  29.0 0.2 fusion.77
  29.2 0.2 fusion.40
  29.4 8.5 %all-to-all-done = f32[8,1,8192]{2,1,0:T(1,128)S(1)} async-done(((f32[8,1,8192]{2,1,0:T(1,128)}), f32[8,1,8192]{2,1,0:T(1,128)S(1)}, u32[]{:S(2)}, u32[]{:S(2)}) %all-to-all-start) | async-done | bytes 262176 | tf_op jit(solution)/shard_map/all_to_all | solution.py:60
  37.8 0.5 broadcast.967
  38.3 1.2 reduce.8
  39.5 2.8 %reshape.676 = f32[512,2,4,16]{3,2,1,0:T(4,128)} reshape(f32[8,8192]{1,0:T(8,128)S(1)} %reduce.8) | data formatting | bytes 524288
  42.3 1.9 %copy.103 = f32[2,16,4,8,64]{4,1,2,3,0:T(8,128)S(1)} copy(f32[2,16,4,8,64]{1,2,0,4,3:T(4,128)} %bitcast.191) | data formatting | bytes 524288 | tf_op jit(solution)/shard_map/all_to_all | solution.py:60
  44.2 0.7 convolution_bitcast_fusion.4
  44.9 2.2 %convolution_bitcast_fusion.2 = f32[2,32,32,64]{3,1,2,0:T(8,128)} fusion(f32[2,16,32,64]{3,2,1,0:T(8,128)S(1)} %convolution_bitcast_fusion.4, f32[16,32]{1,0:T(8,128)S(1)} %copy-done.1), kind=kOutput, calls=%fused_computation.18 | convolution fusion | flops 25165824 | bytes 788480 | tf_op jit(solution)/shard_map/qckm,cr->qrkm/dot_general | solution.py:62
  47.1 0.0 reduce-scatter.2.cloned.1.call-update
  47.2 0.2 all-reduce.2.cloned.1.call-start
  47.4 0.2 fusion.41
  47.6 0.1 copy.39
  47.7 0.1 reshape.644
  47.8 0.1 dynamic_slice.3
  47.9 0.0 copy-start.4
  47.9 3.7 %convolution_bitcast_fusion.1 = f32[2,8,32,8,64]{4,2,3,1,0:T(8,128)S(1)} fusion(f32[2,8,32,8,8,4]{2,5,4,3,1,0:T(4,128)S(1)} %copy-done, f32[64,8]{0,1:T(8,128)S(1)} %fusion.40, f32[64,4]{0,1:T(4,128)S(1)} %fusion.41), kind=kOutput, calls=%fused_computation.17 | convolution fusion | flops 100665344 | bytes 1575936 | tf_op jit(solution)/shard_map/prsabe,mb,me->prsam/dot_general | solution.py:74
  51.6 0.1 compare_convert_fusion
  51.7 9.0 %convolution_bitcast_fusion = f32[2,8,32,32,64]{4,3,2,1,0:T(8,128)} fusion(f32[2,8,32,8,64]{4,2,3,1,0:T(8,128)S(1)} %convolution_bitcast_fusion.1, f32[32,8]{0,1:T(8,128)S(1)} %copy-done.4), kind=kOutput, calls=%fused_computation.9 | convolution fusion | flops 100663296 | bytes 5243904 | tf_op jit(solution)/shard_map/prsam,ka->prskm/dot_general | solution.py:75
  60.7 10.5 %reduce-scatter.2.cloned.1.call-done = f32[2,8,32,64]{3,1,2,0:T(8,128)} async-done(((f32[2,32,32,64]{3,1,2,0:T(8,128)}), f32[2,8,32,64]{3,1,2,0:T(8,128)}) %reduce-scatter.2.cloned.1.call-update) | async-done | bytes 131088 | tf_op jit(solution)/shard_map/reduce_scatter | solution.py:63
  71.2 1.0 broadcast_multiply_fusion
  72.3 4.6 %multiply_reduce_fusion.3 = (f32[32,64,32]{1,0,2:T(8,128)S(1)}, f32[32,64,32]{1,0,2:T(8,128)S(1)}, f32[32,64,32]{1,0,2:T(8,128)S(1)}, f32[32,64,32]{1,0,2:T(8,128)S(1)}) fusion(f32[2,8,32,32,64]{4,3,2,1,0:T(8,128)} %convolution_bitcast_fusion, f32[32,64,8]{1,0,2:T(8,128)S(1)} %copy.107, f32[32,64,8]{1,0,2:T(8,128)S(1)} %copy.108), kind=kLoop, calls=%fused_computation.8 | loop fusion | flops 3932160 | bytes 5373952
  76.9 0.6 fusion.15
  77.5 0.6 fusion.14
  78.1 1.1 pad_maximum_fusion
  79.2 0.0 all-reduce.2.cloned.1.call-update
  79.2 36.5 %all-reduce.2.cloned.1.call-done = f32[2,32,32,64]{3,1,2,0:T(8,128)} async-done(((f32[2,32,32,64]{3,1,2,0:T(8,128)}), f32[2,32,32,64]{3,1,2,0:T(8,128)}) %all-reduce.2.cloned.1.call-update) | async-done | bytes 524304 | tf_op jit(solution)/shard_map/psum | solution.py:82
  115.7 1.9 %convolution_bitcast_fusion.5 = f32[2,16,32,64]{3,1,2,0:T(8,128)S(1)} fusion(f32[2,32,32,64]{3,1,2,0:T(8,128)} %all-reduce.2.cloned.1.call-done, f32[16,32]{1,0:T(8,128)S(1)} %copy-done.2), kind=kOutput, calls=%fused_computation.22 | convolution fusion | flops 25165824 | bytes 788480 | tf_op jit(solution)/shard_map/os,qskm->qokm/dot_general | solution.py:83
  117.6 0.7 convolution_bitcast_fusion.3
  118.3 0.3 copy.140
  118.6 1.0 reshape.677
  119.6 5.5 %all-to-all-start.1 = ((f32[8,1,8192]{2,1,0:T(1,128)}), f32[8,1,8192]{2,1,0:T(1,128)S(1)}, u32[]{:S(2)}, u32[]{:S(2)}) async-start(f32[8,1,8192]{2,1,0:T(1,128)} %reshape.677), calls=%async_computation.2 | async-start | bytes 524288 | tf_op jit(solution)/shard_map/all_to_all | solution.py:86
  125.2 0.1 cosine_multiply_fusion.2
  125.2 8.4 %all-to-all-done.1 = f32[8,1,8192]{2,1,0:T(1,128)S(1)} async-done(((f32[8,1,8192]{2,1,0:T(1,128)}), f32[8,1,8192]{2,1,0:T(1,128)S(1)}, u32[]{:S(2)}, u32[]{:S(2)}) %all-to-all-start.1) | async-done | bytes 262176 | tf_op jit(solution)/shard_map/all_to_all | solution.py:86
  133.6 1.2 reduce.9
  134.8 0.2 reshape.678
  135.0 0.3 copy.139
  135.3 1.8 %reshape.645 = f32[2,16,4,32,16]{4,3,2,1,0:T(8,128)} reshape(f32[2,16,4,8,64]{4,3,2,1,0:T(8,128)S(1)} %bitcast.194) | data formatting | bytes 524288 | tf_op jit(solution)/shard_map/reshape | solution.py:87
  137.1 5.1 %fusion.3 = f32[256,2,16,4,16,1]{0,4,1,5,3,2:T(8,128)S(1)} fusion(f32[256,1,2,32]{0,3,2,1:T(8,128)S(1)} %get-tuple-element.16, f32[256,1,2,32]{0,3,2,1:T(8,128)S(1)} %get-tuple-element.13, f32[2,16,4,32,16]{4,3,2,1,0:T(8,128)} %reshape.645), kind=kOutput, calls=%fused_computation.11 | convolution fusion | flops 402685952 | bytes 2490368 | tf_op jit(solution)/shard_map/pcxjl,ypqj->cxqly/dot_general | solution.py:89
  142.2 14.9 %bitcast_convert_fusion = bf16[16,4,256,128]{3,2,1,0:T(8,128)(2,1)} fusion(f32[256,2,16,4,16,1]{0,4,1,5,3,2:T(8,128)S(1)} %fusion.3, f32[1,16,128]{2,1,0:T(8,128)S(1)} %get-tuple-element.22, f32[1,16,128]{2,1,0:T(8,128)S(1)} %get-tuple-element.21), kind=kOutput, calls=%fused_computation | convolution fusion | flops 807407616 | bytes 6307840 | tf_op jit(solution)/shard_map/cxqly,qlz->cxyz/dot_general | solution.py:90
  (22 shorter events, 0.2 us)
Async XLA Ops:
  6.5 41.3 %copy-start = (f32[2,8,32,8,8,4]{2,5,4,3,1,0:T(4,128)S(1)}, f32[2,8,32,8,8,4]{2,5,4,3,1,0:T(4,128)}, u32[]{:S(2)}) copy-start(f32[2,8,32,8,8,4]{2,5,4,3,1,0:T(4,128)} %param.9) | copy-start | bytes 1572868
  17.9 11.3 %copy-start.5 = (f32[32,8]{0,1:T(8,128)S(1)}, f32[32,8]{0,1:T(8,128)}, u32[]{:S(2)}) copy-start(f32[32,8]{0,1:T(8,128)} %param.13) | copy-start | bytes 3076
  21.6 16.2 %all-to-all-start = ((f32[8,1,8192]{2,1,0:T(1,128)}), f32[8,1,8192]{2,1,0:T(1,128)S(1)}, u32[]{:S(2)}, u32[]{:S(2)}) async-start(f32[8,1,8192]{2,1,0:T(1,128)} %reshape.675), calls=%async_computation | async-start | bytes 524288 | tf_op jit(solution)/shard_map/all_to_all | solution.py:60
  28.9 42.3 %reduce-scatter.2.cloned.1.call-start = ((), (), s32[]{:S(2)}) async-start(), calls=%async_computation.3 | async-start | bytes 1310720 | tf_op jit(solution)/shard_map/reduce_scatter | solution.py:63
  42.3 2.6 %copy-start.1 = (f32[16,32]{1,0:T(8,128)S(1)}, f32[16,32]{1,0:T(8,128)}, u32[]{:S(2)}) copy-start(f32[16,32]{1,0:T(8,128)} %param.10) | copy-start | bytes 6148
  44.2 3.2 %copy-start.6 = (f32[16,4]{0,1:T(4,128)S(1)}, f32[16,4]{0,1:T(4,128)}, u32[]{:S(2)}) copy-start(f32[16,4]{0,1:T(4,128)} %param.14) | copy-start | bytes 772
  44.2 3.4 %copy-start.3 = (s32[32,16]{0,1:T(8,128)S(1)}, s32[32,16]{0,1:T(8,128)}, u32[]{:S(2)}) copy-start(s32[32,16]{0,1:T(8,128)} %param.15) | copy-start | bytes 6148
  47.2 68.5 %all-reduce.2.cloned.1.call-start = ((), (), s32[]{:S(2)}) async-start(), calls=%async_computation.4 | async-start | bytes 2097152 | tf_op jit(solution)/shard_map/psum | solution.py:82
  47.9 3.8 %copy-start.4 = (f32[32,8]{0,1:T(8,128)S(1)}, f32[32,8]{0,1:T(8,128)}, u32[]{:S(2)}) copy-start(f32[32,8]{0,1:T(8,128)} %param.12) | copy-start | bytes 3076
  77.5 38.2 %copy-start.2 = (f32[16,32]{1,0:T(8,128)S(1)}, f32[16,32]{1,0:T(8,128)}, u32[]{:S(2)}) copy-start(f32[16,32]{1,0:T(8,128)} %param.11) | copy-start | bytes 6148
  119.6 14.0 %all-to-all-start.1 = ((f32[8,1,8192]{2,1,0:T(1,128)}), f32[8,1,8192]{2,1,0:T(1,128)S(1)}, u32[]{:S(2)}, u32[]{:S(2)}) async-start(f32[8,1,8192]{2,1,0:T(1,128)} %reshape.677), calls=%async_computation.2 | async-start | bytes 524288 | tf_op jit(solution)/shard_map/all_to_all | solution.py:86
Sparse Core Ops, SparseCore 0:
  47.3 23.8 reduce-scatter.1
  79.3 36.2 all-reduce.1
where the time goes:
time: 164 us
  waiting for transfers between devices  63.9 us (39%)
  matrix products  46.9 us (29%)
  local copies, waits for them, and re-layouts  15.6 us (10%)
  between operations  13.6 us (8%)
  starting transfers between devices  13.1 us (8%)
  other arithmetic  10.8 us (7%)
    psum x1, waiting for transfers between devices, per_device(): mixed_sum = lax.psum(jnp.stack([mixed_re, mixed_im]), 'col')  36.5 us
    dot_general x1, matrix products, per_device(): jnp.einsum('cxqly,qlz->cxyz', y_values, z_backward, precision=highest)  14.9 us
    reduce_scatter x1, waiting for transfers between devices, per_device(): lax.psum_scatter(partial_value, 'col', scatter_dimension=1, tiled=True)  10.5 us
    dot_general x1, matrix products, per_device(): jnp.einsum('prsam,ka->prskm', core_cols, x_factor, precision=highest)  9.02 us
    all_to_all x1, waiting for transfers between devices, per_device(): lax.all_to_all(y_spectrum, 'gx', split_axis=3, concat_axis=2, tiled=True)  8.47 us
    all_to_all x1, waiting for transfers between devices, per_device(): lax.all_to_all(x_values, 'gx', split_axis=2, concat_axis=3, tiled=True)  8.4 us
    unnamed x22, local copies, waits for them, and re-layouts  7.99 us
    all_to_all x1, starting transfers between devices, per_device(): lax.all_to_all(y_spectrum, 'gx', split_axis=3, concat_axis=2, tiled=True)  7.29 us
  transfers between devices with their start and end apart: 4, of which 4 were waited for; matrix products, arithmetic and copies ran while one was open for 8% of the time, Pallas kernels for 0%

commit v1 on v0

--- a/solution.py
+++ b/solution.py
@@ -1,9 +1,18 @@
+import functools
 import math
 
 import jax
 import jax.numpy as jnp
+import numpy as np
 from jax import lax
+from jax.experimental import pallas as pl
+from jax.experimental.pallas import tpu as pltpu
 from jax.sharding import PartitionSpec as P
+
+MESH = pl.DeviceIdType.MESH
+VMEM = pl.BlockSpec(memory_space=pltpu.VMEM)
+F32 = jnp.float32
+BF16 = jnp.bfloat16
 
 
 def slot_freq(slot_count):
@@ -34,7 +43,7 @@
     return (forward, backward)
 
 
-def per_device(
+def plain_device(
     grid_field, tucker_core, in_factor, out_factor, x_factor, y_factor, z_factor, kx_reach
 ):
     highest = lax.Precision.HIGHEST
@@ -91,6 +100,409 @@
     return result.astype(jnp.bfloat16)
 
 
+def split_np(table):
+    high = table.astype(np.float32).astype(BF16)
+    low = (table - high.astype(np.float64)).astype(np.float32).astype(BF16)
+    return high, low
+
+
+def split(values):
+    high = values.astype(BF16)
+    return high, (values - high.astype(F32)).astype(BF16)
+
+
+def freqs(slots):
+    index = np.arange(slots)
+    return np.where(index < slots // 2, index, index - slots)
+
+
+def waves(extent, frequencies):
+    steps = np.arange(extent)[:, None] * frequencies[None, :] % extent
+    angle = 2.0 * np.pi / extent * steps
+    return np.cos(angle) / math.sqrt(extent), np.sin(angle) / math.sqrt(extent)
+
+
+def dot(a, b):
+    return jnp.dot(a, b, preferred_element_type=F32)
+
+
+def forward_tables(grid_y, grid_z, modes_y, modes_z, planes):
+    cos_y, sin_y = waves(grid_y, freqs(modes_y))
+    high, low = split_np(np.concatenate([cos_y.T, -sin_y.T], 0))
+    y_table = np.concatenate([high, low], 0)
+    cos_z, sin_z = waves(grid_z, np.arange(modes_z))
+    table = np.zeros((planes, 2, grid_z, modes_z, planes, 2))
+    for plane in range(planes):
+        table[plane, 0, :, :, plane, 0] = cos_z
+        table[plane, 0, :, :, plane, 1] = -sin_z
+        table[plane, 1, :, :, plane, 0] = sin_z
+        table[plane, 1, :, :, plane, 1] = cos_z
+    high, low = split_np(table.reshape(planes * 2 * grid_z, -1))
+    return y_table, np.concatenate([high, low], 1)
+
+
+def inverse_tables(grid_y, grid_z, modes_y, modes_z, planes):
+    cos_y, sin_y = waves(grid_y, freqs(modes_y))
+    high, low = split_np(np.concatenate([cos_y, -sin_y], 1))
+    y_table = np.concatenate([high, high, low], 1)
+    cos_z, sin_z = waves(grid_z, np.arange(modes_z))
+    weight = np.where(np.arange(modes_z) == 0, 1.0, 2.0)
+    cos_z, sin_z = (cos_z * weight).T, (sin_z * weight).T
+    table = np.zeros((modes_z, planes, 2, planes, 2, grid_z))
+    for plane in range(planes):
+        table[:, plane, 0, plane, 0, :] = cos_z
+        table[:, plane, 1, plane, 0, :] = -sin_z
+        table[:, plane, 0, plane, 1, :] = sin_z
+        table[:, plane, 1, plane, 1, :] = cos_z
+    high, low = split_np(table.reshape(modes_z * planes * 2, -1))
+    return y_table, high, low
+
+
+def x_tables(grid_x, modes_x):
+    cos_x, sin_x = waves(grid_x, freqs(modes_x))
+    real = np.stack([cos_x.T, sin_x.T], 2).reshape(modes_x, -1)
+    imag = np.stack([-sin_x.T, cos_x.T], 2).reshape(modes_x, -1)
+    high, low = split_np(np.concatenate([real, imag, -imag, real], 0))
+    forward = np.concatenate([high, high, low], 1)
+    real = np.concatenate([cos_x, -sin_x], 1)
+    imag = np.concatenate([sin_x, cos_x], 1)
+    high, low = split_np(np.stack([real, imag], 1).reshape(grid_x * 2, -1))
+    backward = np.concatenate([high, high, low], 1)
+    return forward, backward
+
+
+def forward_kernel(field_ref, y_ref, z_ref, out_ref, high_ref, low_ref):
+    channel = pl.program_id(0)
+    channels = pl.num_programs(0)
+    planes, modes_y = field_ref.shape[1], out_ref.shape[0]
+    half = 2 * modes_y
+    parts = []
+    for plane in range(planes):
+        both = dot(y_ref[...], field_ref[0, plane])
+        y_values = both[:half] + both[half:]
+        parts += [y_values[:modes_y], y_values[modes_y:]]
+    high, low = split(jnp.concatenate(parts, 1))
+    rows = pl.ds(pl.multiple_of(channel * modes_y, modes_y), modes_y)
+    high_ref[rows] = high
+    low_ref[rows] = low
+
+    @pl.when(channel == channels - 1)
+    def _():
+        lanes = out_ref.shape[2]
+        both = dot(high_ref[...], z_ref[...])
+        result = both[:, :lanes] + both[:, lanes:] + dot(low_ref[...], z_ref[:, :lanes])
+        out_ref[...] = jnp.swapaxes(result.reshape(-1, modes_y, lanes), 0, 1)
+
+
+def forward(grid_field, modes_y, modes_z):
+    channels, planes, grid_y, grid_z = grid_field.shape
+    y_table, z_table = forward_tables(grid_y, grid_z, modes_y, modes_z, planes)
+    lanes = planes * 2 * modes_z
+    wide = planes * 2 * grid_z
+    return pl.pallas_call(
+        forward_kernel,
+        grid=(channels,),
+        in_specs=[
+            pl.BlockSpec((1, planes, grid_y, grid_z), lambda i: (i, 0, 0, 0)),
+            pl.BlockSpec(y_table.shape, lambda i: (0, 0)),
+            pl.BlockSpec(z_table.shape, lambda i: (0, 0)),
+        ],
+        out_specs=pl.BlockSpec((modes_y, channels, lanes), lambda i: (0, 0, 0)),
+        out_shape=jax.ShapeDtypeStruct((modes_y, channels, lanes), F32),
+        scratch_shapes=[
+            pltpu.VMEM((channels * modes_y, wide), BF16),
+            pltpu.VMEM((channels * modes_y, wide), BF16),
+        ],
+    )(grid_field, jnp.asarray(y_table), jnp.asarray(z_table))
+
+
+def exchange_kernel(width_gx, width_col, with_core, *refs):
+    if with_core:
+        send_ref, core_ref, out_ref, core_out, sends, recvs, own, core_sends, core_recvs, core_own = refs
+    else:
+        send_ref, out_ref, sends, recvs, own = refs
+    count = width_gx * width_col
+    my_gx, my_col = lax.axis_index("gx"), lax.axis_index("col")
+    me = my_gx * width_col + my_col
+    barrier = pltpu.get_barrier_semaphore()
+
+    def where(step):
+        peer = lax.rem(me + step, count)
+        return peer, (peer // width_col, lax.rem(peer, width_col))
+
+    def greet(step, carry):
+        pl.semaphore_signal(barrier, inc=1, device_id=where(step)[1], device_id_type=MESH)
+        return carry
+
+    lax.fori_loop(1, count, greet, 0)
+    keep = pltpu.make_async_copy(send_ref.at[me], out_ref.at[me], own)
+    keep.start()
+    if with_core:
+        core_keep = pltpu.make_async_copy(core_ref.at[my_col], core_out.at[my_col], core_own)
+        core_keep.start()
+    pl.semaphore_wait(barrier, count - 1)
+
+    def block(step):
+        peer, place = where(step)
+        return pltpu.make_async_remote_copy(
+            src_ref=send_ref.at[peer],
+            dst_ref=out_ref.at[me],
+            send_sem=sends.at[step],
+            recv_sem=recvs.at[step],
+            device_id=place,
+            device_id_type=MESH,
+        )
+
+    def core_block(step):
+        peer = lax.rem(my_col + step, width_col)
+        return pltpu.make_async_remote_copy(
+            src_ref=core_ref.at[peer],
+            dst_ref=core_out.at[my_col],
+            send_sem=core_sends.at[step],
+            recv_sem=core_recvs.at[step],
+            device_id=(my_gx, peer),
+            device_id_type=MESH,
+        )
+
+    def start(step, carry):
+        block(step).start()
+        return carry
+
+    lax.fori_loop(1, count, start, 0)
+    if with_core:
+        for step in range(1, width_col):
+            core_block(step).start()
+
+    def finish(step, carry):
+        block(step).wait_send()
+        source = lax.rem(me + count - step, count)
+        pltpu.make_async_remote_copy(
+            src_ref=send_ref.at[source],
+            dst_ref=out_ref.at[source],
+            send_sem=sends.at[step],
+            recv_sem=recvs.at[step],
+            device_id=(my_gx, my_col),
+            device_id_type=MESH,
+        ).wait_recv()
+        return carry
+
+    lax.fori_loop(1, count, finish, 0)
+    keep.wait()
+    if with_core:
+        for step in range(1, width_col):
+            core_block(step).wait_send()
+            source = lax.rem(my_col + width_col - step, width_col)
+            pltpu.make_async_remote_copy(
+                src_ref=core_ref.at[source],
+                dst_ref=core_out.at[source],
+                send_sem=core_sends.at[step],
+                recv_sem=core_recvs.at[step],
+                device_id=(my_gx, my_col),
+                device_id_type=MESH,
+            ).wait_recv()
+        core_keep.wait()
+
+
+def exchange(width_gx, width_col, collective, *arrays):
+    with_core = len(arrays) == 2
+    count = width_gx * width_col
+    dma = pltpu.SemaphoreType.DMA
+    scratch = [dma((count,)), dma((count,)), dma]
+    if with_core:
+        scratch += [dma((width_col,)), dma((width_col,)), dma]
+    return pl.pallas_call(
+        functools.partial(exchange_kernel, width_gx, width_col, with_core),
+        out_shape=[jax.ShapeDtypeStruct(a.shape, a.dtype) for a in arrays],
+        in_specs=[VMEM] * len(arrays),
+        out_specs=[VMEM] * len(arrays),
+        scratch_shapes=scratch,
+        compiler_params=pltpu.CompilerParams(collective_id=collective, has_side_effects=True),
+    )(*arrays)
+
+
+def middle_kernel(
+    width_gx, modes_z, arrived_ref, core_ref, x_rows_ref, mask_ref, z_rows_ref, fore_ref, back_ref,
+    out_ref, rank_ref, high_ref, low_ref, plane_ref,
+):
+    width_col, channels = core_ref.shape[0], arrived_ref.shape[1]
+    lanes = arrived_ref.shape[2]
+    lead = lanes // modes_z
+    both_modes = back_ref.shape[1] // 3
+    ranks = x_rows_ref.shape[1]
+    core_rows = ranks // width_col
+
+    def core_part(first, rows):
+        return core_ref[:, first : first + rows, :].reshape(width_col * rows, lanes)
+
+    at = 2 * core_rows
+    in_rows = jnp.concatenate([core_part(at, channels), core_part(at + channels, channels)], 1)
+    out_rows = core_part(at + 2 * channels, channels)
+    in_high, in_low = split(in_rows)
+    in_stack = jnp.concatenate([in_high, in_low, in_high], 0)
+    for slab in range(width_gx):
+        block = arrived_ref[slab * width_col : (slab + 1) * width_col].reshape(-1, lanes)
+        high = block.astype(BF16).astype(F32)
+        stacked = jnp.concatenate([high, high, block - high], 0)
+        value = dot(stacked.T.astype(BF16), in_stack)
+        rank_ref[:, slab * lead : (slab + 1) * lead, :] = value.reshape(modes_z, lead, ranks)
+    for l in range(modes_z):
+        high, low = split(rank_ref[l])
+        value = dot(fore_ref[...], jnp.concatenate([high, low, high], 0))
+        value = value * x_rows_ref[...] * mask_ref[:, l : l + 1]
+        value = jnp.concatenate([value[:both_modes], value[both_modes:]], 1)
+        rows = slice(l * both_modes, (l + 1) * both_modes)
+        high_ref[rows], low_ref[rows] = split(value)
+    core = jnp.concatenate([core_part(0, core_rows), core_part(core_rows, core_rows)], 0)
+    core_high, core_low = split(core)
+    both = dot(high_ref[...], jnp.concatenate([core_high, core_low], 1))
+    mixed = both[:, :lanes] + both[:, lanes:] + dot(low_ref[...], core_high)
+    for l in range(modes_z):
+        value = mixed[l * both_modes : (l + 1) * both_modes] * z_rows_ref[l : l + 1]
+        high, low = split(value)
+        value = dot(back_ref[...], jnp.concatenate([high, low, high], 0))
+        plane_ref[:, l] = value.reshape(width_gx, lead, lanes)
+    out_high, out_low = split(out_rows)
+    out_stack = jnp.concatenate([out_high, out_low], 0)
+    count = out_high.shape[0]
+    last = (((1,), (1,)), ((), ()))
+    for slab in range(width_gx):
+        high, low = split(plane_ref[slab].reshape(lanes, lanes))
+        both = lax.dot_general(out_stack, high, last, preferred_element_type=F32)
+        value = both[:count] + both[count:]
+        value = value + lax.dot_general(out_high, low, last, preferred_element_type=F32)
+        out_ref[slab * width_col : (slab + 1) * width_col] = value.reshape(
+            width_col, channels, lanes
+        )
+
+
+def middle(arrived, cores, x_rows, mask, z_rows, grid_x, modes_x, modes_z, width_gx):
+    fore, back = x_tables(grid_x, modes_x)
+    lanes = arrived.shape[2]
+    ranks = x_rows.shape[1]
+    return pl.pallas_call(
+        functools.partial(middle_kernel, width_gx, modes_z),
+        out_shape=jax.ShapeDtypeStruct(arrived.shape, F32),
+        in_specs=[VMEM] * 7,
+        out_specs=VMEM,
+        scratch_shapes=[
+            pltpu.VMEM((modes_z, 2 * grid_x, ranks), F32),
+            pltpu.VMEM((modes_z * 2 * modes_x, 2 * ranks), BF16),
+            pltpu.VMEM((modes_z * 2 * modes_x, 2 * ranks), BF16),
+            pltpu.VMEM((width_gx, modes_z, lanes // modes_z, lanes), F32),
+        ],
+    )(arrived, cores, x_rows, mask, z_rows, jnp.asarray(fore), jnp.asarray(back))
+
+
+def inverse_kernel(spec_ref, y_ref, z_high_ref, z_low_ref, out_ref, high_ref, low_ref):
+    channel = pl.program_id(0)
+    modes_y, _, lanes = spec_ref.shape
+    planes, grid_z = out_ref.shape[1], out_ref.shape[3]
+
+    @pl.when(channel == 0)
+    def _():
+        values = jnp.swapaxes(spec_ref[...], 0, 1).reshape(-1, lanes)
+        high, low = split(values)
+        result = dot(high, z_high_ref[...]) + dot(high, z_low_ref[...])
+        result = result + dot(low, z_high_ref[...])
+        high_ref[...], low_ref[...] = split(result)
+
+    rows = pl.ds(pl.multiple_of(channel * modes_y, modes_y), modes_y)
+    high, low = high_ref[rows], low_ref[rows]
+
+    def tall(values, plane):
+        at = 2 * plane * grid_z
+        return [values[:, at : at + grid_z], values[:, at + grid_z : at + 2 * grid_z]]
+
+    stacks = []
+    for plane in range(planes):
+        high_part = tall(high, plane)
+        stacks.append(jnp.concatenate(high_part + tall(low, plane) + high_part, 0))
+    for plane in range(0, planes, 2):
+        pair = stacks[plane : plane + 2]
+        value = dot(y_ref[...], jnp.concatenate(pair, 1)).astype(BF16)
+        for step in range(len(pair)):
+            out_ref[0, plane + step] = value[:, step * grid_z : (step + 1) * grid_z]
+
+
+def inverse(returned, planes, grid_y, grid_z, modes_z):
+    modes_y, channels, _ = returned.shape
+    y_table, z_high, z_low = inverse_tables(grid_y, grid_z, modes_y, modes_z, planes)
+    wide = planes * 2 * grid_z
+    return pl.pallas_call(
+        inverse_kernel,
+        grid=(channels,),
+        in_specs=[
+            pl.BlockSpec(returned.shape, lambda i: (0, 0, 0)),
+            pl.BlockSpec(y_table.shape, lambda i: (0, 0)),
+            pl.BlockSpec(z_high.shape, lambda i: (0, 0)),
+            pl.BlockSpec(z_low.shape, lambda i: (0, 0)),
+        ],
+        out_specs=pl.BlockSpec((1, planes, grid_y, grid_z), lambda i: (i, 0, 0, 0)),
+        out_shape=jax.ShapeDtypeStruct((channels, planes, grid_y, grid_z), BF16),
+        scratch_shapes=[
+            pltpu.VMEM((channels * modes_y, wide), BF16),
+            pltpu.VMEM((channels * modes_y, wide), BF16),
+        ],
+    )(returned, jnp.asarray(y_table), jnp.asarray(z_high), jnp.asarray(z_low))
+
+
+def row_device(
+    grid_field, tucker_core, in_factor, out_factor, x_factor, y_factor, z_factor, kx_reach
+):
+    channels, planes, grid_y, grid_z = grid_field.shape
+    modes_x, modes_y, modes_z = x_factor.shape[0], y_factor.shape[0], z_factor.shape[0]
+    width_gx, width_col = lax.axis_size("gx"), lax.axis_size("col")
+    slab = lax.axis_index("gx")
+    row = slab * width_col + lax.axis_index("col")
+    rank_out = out_factor.shape[1]
+    rank_dev, rank_x, rank_z = tucker_core.shape[1], x_factor.shape[1], z_factor.shape[1]
+    spectrum = forward(grid_field, modes_y, modes_z)
+    y_rows = lax.dynamic_slice_in_dim(y_factor, slab * width_col, width_col)
+    core = jnp.einsum("prsabe,db->dpares", tucker_core, y_rows, precision=lax.Precision.HIGHEST)
+    core = core.reshape(width_col, 2 * rank_x * rank_dev, rank_z * rank_out)
+    lanes = core.shape[2]
+    in_wide = in_factor.reshape(channels, width_col, 1, rank_dev)
+    in_wide = jnp.broadcast_to(in_wide, (channels, width_col, rank_x, rank_dev))
+    in_wide = in_wide.reshape(channels, 2, lanes).swapaxes(0, 1).reshape(2 * channels, lanes)
+    out_wide = jnp.tile(out_factor, (1, rank_z))
+    factors = jnp.concatenate([in_wide, out_wide], 0)
+    factors = jnp.broadcast_to(factors[None], (width_col,) + factors.shape)
+    message = jnp.concatenate([core, factors], 1)
+    arrived, cores = exchange(width_gx, width_col, 0, spectrum, message)
+    x_rows = jnp.broadcast_to(x_factor[:, None, :, None], (modes_x, width_col, rank_x, rank_dev))
+    x_rows = jnp.tile(x_rows.reshape(modes_x, -1), (4, 1))
+    reach = lax.dynamic_slice_in_dim(kx_reach, row, 1)
+    mask = (jnp.abs(slot_freq(modes_x))[:, None] < reach).astype(F32)
+    z_rows = jnp.repeat(z_factor, rank_out, axis=1)
+    sent = middle(
+        arrived, cores, x_rows, jnp.tile(mask, (4, 1)), z_rows, planes * width_gx, modes_x,
+        modes_z, width_gx,
+    )
+    (returned,) = exchange(width_gx, width_col, 1, sent)
+    return inverse(returned, planes, grid_y, grid_z, modes_z)
+
+
+def per_device(
+    grid_field, tucker_core, in_factor, out_factor, x_factor, y_factor, z_factor, kx_reach
+):
+    planes, grid_z = grid_field.shape[1], grid_field.shape[3]
+    modes_y, modes_z = y_factor.shape[0], z_factor.shape[0]
+    devices = lax.axis_size("gx") * lax.axis_size("col")
+    ranks = in_factor.shape[1] * x_factor.shape[1]
+    row_each = (
+        devices == modes_y
+        and planes == 4
+        and grid_z == 128
+        and planes * 2 * modes_z == 128
+        and ranks == 256
+        and out_factor.shape[1] * z_factor.shape[1] == 128
+    )
+    device = row_device if row_each else plain_device
+    return device(
+        grid_field, tucker_core, in_factor, out_factor, x_factor, y_factor, z_factor, kx_reach
+    )
+
+
 def solution(mesh):
     return jax.shard_map(
         per_device,

time: 164 us -> 63.7 us (0.39)
  waiting for transfers between devices: 63.9 us -> 0 us
  Pallas kernels: 0 us -> 53 us
  matrix products: 46.9 us -> 1.94 us
  between operations: 13.6 us -> 0.07 us
  starting transfers between devices: 13.1 us -> 0 us
  other arithmetic: 10.8 us -> 0.84 us
  local copies, waits for them, and re-layouts: 15.6 us -> 7 us
    pallas_call x0 -> x5, Pallas kernels: none -> 53 us  [the longest x2 27.8 us: exchange(): pl.pallas_call(functools.partial(exchange_kernel, width_gx, width_col, wi...]
    dot_general x12 -> x1, matrix products: 46.9 us -> 1.94 us  [row_device(): jnp.einsum('prsabe,db->dpares', tucker_core, y_rows, precision=lax.Precis...]
    psum x1 -> x0, waiting for transfers between devices: 36.5 us -> none  [per_device(): mixed_sum = lax.psum(jnp.stack([mixed_re, mixed_im]), 'col')]
    all_to_all x2 -> x0, waiting for transfers between devices: 16.9 us -> none  [the longest x1 8.47 us: per_device(): lax.all_to_all(y_spectrum, 'gx', split_axis=3, concat_axis=2, tiled=True)]
    all_to_all x2 -> x0, starting transfers between devices: 12.8 us -> none  [the longest x1 7.29 us: per_device(): lax.all_to_all(y_spectrum, 'gx', split_axis=3, concat_axis=2, tiled=True)]
    reduce_scatter x1 -> x0, waiting for transfers between devices: 10.5 us -> none  [per_device(): lax.psum_scatter(partial_value, 'col', scatter_dimension=1, tiled=True)]
    unnamed x22 -> x6, local copies, waits for them, and re-layouts: 7.99 us -> 1.54 us
    unnamed x1 -> x0, other arithmetic: 4.65 us -> none
  transfers between devices with their start and end apart: 4 -> 0, of which waited for: 4 -> 0; matrix products, arithmetic and copies ran while one was open for 8% -> 0% of each run, Pallas kernels for 0% -> 0%
where the time goes in v1:
time: 63.7 us; the launch traced here: 62.9 us
  Pallas kernels  53 us (83%)
  local copies, waits for them, and re-layouts  7 us (11%)
  matrix products  1.94 us (3%)
  other arithmetic  0.84 us (1%)
    pallas_call x2, Pallas kernels, exchange(): pl.pallas_call(functools.partial(exchange_kernel, width_gx, width_col, wi...  27.8 us
    pallas_call x1, Pallas kernels, forward(): pl.pallas_call(forward_kernel, grid=(channels,), in_specs=[pl.BlockSpec((...  11.5 us
    pallas_call x1, Pallas kernels, inverse(): pl.pallas_call(inverse_kernel, grid=(channels,), in_specs=[pl.BlockSpec(r...  9.84 us
    pallas_call x1, Pallas kernels, middle(): pl.pallas_call(functools.partial(middle_kernel, width_gx, modes_z), out_s...  3.9 us
    dot_general x1, matrix products, row_device(): jnp.einsum('prsabe,db->dpares', tucker_core, y_rows, precision=lax.Precis...  1.94 us
    unnamed x6, local copies, waits for them, and re-layouts  1.54 us

profile of v1, /device:TPU:0, one launch (start us, length us, event | category | flops | bytes accessed | tf_op | source)
XLA Modules:
  0.0 62.9 jit_solution(17593486244722138298)
XLA Ops:
  0.0 0.0 copy-start
  0.0 1.0 %dynamic-slice_reduce_fusion = s32[16]{0:T(128)S(1)} fusion(s32[32,16]{0,1:T(8,128)} %param.22, s32[]{:T(128)S(6)} %select_n.16), kind=kLoop, calls=%fused_computation.6 | loop fusion | bytes 132 | tf_op jit(solution)/shard_map/dynamic_slice | solution.py:474
  1.0 0.8 %copy.33 = f32[16,4]{1,0:T(8,128)S(1)} copy(f32[16,4]{0,1:T(4,128)} %param.21) | data formatting | bytes 512 | tf_op args[6]
  1.8 0.1 compare_convert_fusion
  1.9 0.8 %copy.30 = f32[16,32]{0,1:T(8,128)S(1)} copy(f32[16,32]{1,0:T(8,128)} %param.17) | data formatting | bytes 4096 | tf_op args[2]
  2.6 0.1 broadcast_in_dim.27
  2.7 0.7 %reshape.67.z_rows_ref = f32[16,128]{1,0:T(8,128)} reshape(f32[16,4,32]{2,1,0:T(4,128)S(1)} %broadcast_in_dim.27) | data formatting | bytes 16384 | tf_op jit(solution)/shard_map/reshape | solution.py:476
  3.4 0.7 %tile.28 = f32[16,4,32]{2,1,0:T(4,128)S(1)} broadcast(f32[16,32]{1,0:T(8,128)} %param.18), dimensions={0,2} | broadcast | bytes 10240 | tf_op jit(solution)/shard_map/tile | solution.py:467
  4.1 0.1 tile.29
  4.2 0.6 tile.33
  4.8 0.1 copy.31
  4.9 0.7 %broadcast_in_dim.26 = f32[32,4,8,8]{0,3,2,1:T(8,128)S(1)} broadcast(f32[32,8]{0,1:T(8,128)} %param.19), dimensions={0,2} | broadcast | bytes 33792 | tf_op jit(solution)/shard_map/broadcast_in_dim | solution.py:472
  5.6 0.1 copy.32
  5.7 0.7 %tile.31 = f32[4,32,256]{2,1,0:T(8,128)} broadcast(f32[32,256]{1,0:T(8,128)S(1)} %copy.32), dimensions={1,2} | broadcast | bytes 163840 | tf_op jit(solution)/shard_map/tile | solution.py:473
  6.4 0.0 copy-start.1
  6.4 11.5 %shard_map.145.refs_0_ = f32[32,16,128]{2,1,0:T(8,128)} custom-call(bf16[16,4,256,128]{3,2,1,0:T(8,128)(2,1)} %field_ref.1, bf16[128,256]{1,0:T(8,128)(2,1)} %constant.34.clone.y_ref, bf16[1024,256]{1,0:T(8,128)(2,1)} %constant.35.clone.z_ref), custom_call_target="tpu_custom_call" | custom-call | tf_op jit(solution)/shard_map/pallas_call | solution.py:202
  17.9 0.0 copy-done
  17.9 0.0 copy-done.1
  17.9 1.9 %fusion.2 = f32[4,2,8,8,4,32]{5,0,4,2,3,1:T(4,128)S(1)} fusion(f32[2,8,32,8,8,4]{2,5,4,3,1,0:T(4,128)S(1)} %copy-done, f32[32,8]{0,1:T(8,128)S(1)} %copy-done.1, s32[]{:T(128)S(6)} %select_n.14), kind=kOutput, calls=%fused_computation.2 | convolution fusion | flops 6291456 | bytes 787460 | tf_op jit(solution)/shard_map/prsabe,db->dpares/dot_general | solution.py:461
  19.8 0.3 copy.29
  20.1 0.5 reshape.64
  20.6 0.8 %pad_maximum_fusion.refs_1_ = f32[4,176,128]{2,1,0:T(8,128)} fusion(f32[4,48,128]{2,1,0:T(8,128)S(1)} %broadcast_in_dim.12, f32[4,128,128]{2,1,0:T(8,128)S(1)} %reshape.64), kind=kLoop, calls=%fused_computation.3 | loop fusion | flops 90112 | bytes 720896 | tf_op jit(solution)/shard_map/concatenate | solution.py:470
  21.3 16.7 %shard_map.146 = (f32[32,16,128]{2,1,0:T(8,128)}, f32[4,176,128]{2,1,0:T(8,128)}) custom-call(f32[32,16,128]{2,1,0:T(8,128)} %shard_map.145.refs_0_, f32[4,176,128]{2,1,0:T(8,128)} %pad_maximum_fusion.refs_1_), custom_call_target="tpu_custom_call" | custom-call | tf_op jit(solution)/shard_map/pallas_call | solution.py:313
  38.1 3.9 %shard_map.147.refs_0_ = f32[32,16,128]{2,1,0:T(8,128)} custom-call(f32[32,16,128]{2,1,0:T(8,128)} %get-tuple-element.7.arrived_ref, f32[4,176,128]{2,1,0:T(8,128)} %get-tuple-element.8.core_ref, f32[128,256]{1,0:T(8,128)} %bitcast.16, f32[128,16]{1,0:T(8,128)} %bitcast.19, f32[16,128]{1,0:T(8,128)} %reshape.67.z_rows_ref, ...), custom_call_target="tpu_custom_call" | custom-call | tf_op jit(solution)/shard_map/pallas_call | solution.py:382
  42.0 11.1 %shard_map.148.spec_ref = f32[32,16,128]{2,1,0:T(8,128)} custom-call(f32[32,16,128]{2,1,0:T(8,128)} %shard_map.147.refs_0_), custom_call_target="tpu_custom_call" | custom-call | tf_op jit(solution)/shard_map/pallas_call | solution.py:313
  53.0 9.8 %shard_map.149 = bf16[16,4,256,128]{3,2,1,0:T(8,128)(2,1)} custom-call(f32[32,16,128]{2,1,0:T(8,128)} %shard_map.148.spec_ref, bf16[256,192]{1,0:T(8,128)(2,1)} %constant.38.clone.y_ref, bf16[128,1024]{1,0:T(8,128)(2,1)} %constant.39.clone.z_high_ref, bf16[128,1024]{1,0:T(8,128)(2,1)} %constant.40.clone.z_low_ref), custom_call_target="tpu_custom_call" | custom-call | tf_op jit(solution)/shard_map/pallas_call | solution.py:431
  (4 shorter events, 0.0 us)
Async XLA Ops:
  0.0 17.9 %copy-start = (f32[2,8,32,8,8,4]{2,5,4,3,1,0:T(4,128)S(1)}, f32[2,8,32,8,8,4]{2,5,4,3,1,0:T(4,128)}, u32[]{:S(2)}) copy-start(f32[2,8,32,8,8,4]{2,5,4,3,1,0:T(4,128)} %param.16) | copy-start | bytes 1572868
  6.4 11.5 %copy-start.1 = (f32[32,8]{0,1:T(8,128)S(1)}, f32[32,8]{0,1:T(8,128)}, u32[]{:S(2)}) copy-start(f32[32,8]{0,1:T(8,128)} %param.20) | copy-start | bytes 3076

commit v2 on v0

--- a/solution.py
+++ b/solution.py
@@ -1,9 +1,18 @@
+import functools
 import math
 
 import jax
 import jax.numpy as jnp
+import numpy as np
 from jax import lax
+from jax.experimental import pallas as pl
+from jax.experimental.pallas import tpu as pltpu
 from jax.sharding import PartitionSpec as P
+
+MESH = pl.DeviceIdType.MESH
+VMEM = pl.BlockSpec(memory_space=pltpu.VMEM)
+F32 = jnp.float32
+BF16 = jnp.bfloat16
 
 
 def slot_freq(slot_count):
@@ -34,7 +43,7 @@
     return (forward, backward)
 
 
-def per_device(
+def plain_device(
     grid_field, tucker_core, in_factor, out_factor, x_factor, y_factor, z_factor, kx_reach
 ):
     highest = lax.Precision.HIGHEST
@@ -91,6 +100,479 @@
     return result.astype(jnp.bfloat16)
 
 
+def split_np(table):
+    high = table.astype(np.float32).astype(BF16)
+    low = (table - high.astype(np.float64)).astype(np.float32).astype(BF16)
+    return high, low
+
+
+def split(values):
+    high = values.astype(BF16)
+    return high, (values - high.astype(F32)).astype(BF16)
+
+
+def freqs(slots):
+    index = np.arange(slots)
+    return np.where(index < slots // 2, index, index - slots)
+
+
+def waves(extent, frequencies):
+    steps = np.arange(extent)[:, None] * frequencies[None, :] % extent
+    angle = 2.0 * np.pi / extent * steps
+    return np.cos(angle) / math.sqrt(extent), np.sin(angle) / math.sqrt(extent)
+
+
+def dot(a, b):
+    return jnp.dot(a, b, preferred_element_type=F32)
+
+
+def forward_tables(grid_y, grid_z, modes_y, modes_z, planes):
+    cos_y, sin_y = waves(grid_y, freqs(modes_y))
+    high, low = split_np(np.concatenate([cos_y.T, -sin_y.T], 0))
+    y_table = np.concatenate([high, low], 0)
+    cos_z, sin_z = waves(grid_z, np.arange(modes_z))
+    table = np.zeros((planes, 2, grid_z, modes_z, planes, 2))
+    for plane in range(planes):
+        table[plane, 0, :, :, plane, 0] = cos_z
+        table[plane, 0, :, :, plane, 1] = -sin_z
+        table[plane, 1, :, :, plane, 0] = sin_z
+        table[plane, 1, :, :, plane, 1] = cos_z
+    high, low = split_np(table.reshape(planes * 2 * grid_z, -1))
+    return y_table, np.concatenate([high, low], 1)
+
+
+def inverse_tables(grid_y, grid_z, modes_y, modes_z, planes):
+    cos_y, sin_y = waves(grid_y, freqs(modes_y))
+    high, low = split_np(np.concatenate([cos_y, -sin_y], 1))
+    y_table = np.concatenate([high, high, low], 1)
+    cos_z, sin_z = waves(grid_z, np.arange(modes_z))
+    weight = np.where(np.arange(modes_z) == 0, 1.0, 2.0)
+    cos_z, sin_z = (cos_z * weight).T, (sin_z * weight).T
+    table = np.zeros((modes_z, planes, 2, planes, 2, grid_z))
+    for plane in range(planes):
+        table[:, plane, 0, plane, 0, :] = cos_z
+        table[:, plane, 1, plane, 0, :] = -sin_z
+        table[:, plane, 0, plane, 1, :] = sin_z
+        table[:, plane, 1, plane, 1, :] = cos_z
+    high, low = split_np(table.reshape(modes_z * planes * 2, -1))
+    return y_table, high, low
+
+
+def x_tables(grid_x, modes_x):
+    cos_x, sin_x = waves(grid_x, freqs(modes_x))
+    real = np.stack([cos_x.T, sin_x.T], 2).reshape(modes_x, -1)
+    imag = np.stack([-sin_x.T, cos_x.T], 2).reshape(modes_x, -1)
+    high, low = split_np(np.concatenate([real, imag, -imag, real], 0))
+    forward = np.concatenate([high, high, low], 1)
+    real = np.concatenate([cos_x, -sin_x], 1)
+    imag = np.concatenate([sin_x, cos_x], 1)
+    high, low = split_np(np.stack([real, imag], 1).reshape(grid_x * 2, -1))
+    backward = np.concatenate([high, high, low], 1)
+    return forward, backward
+
+
+def selectors(width_col, rank_x, rank_dev, rank_z, rank_out):
+    wide = np.arange(width_col * rank_x * rank_dev)
+    rank_in = wide // (rank_x * rank_dev) * rank_dev + wide % rank_dev
+    x_pick = wide // rank_dev % rank_x == np.arange(rank_x)[:, None]
+    in_pick = rank_in == np.arange(width_col * rank_dev)[:, None]
+    slim = np.arange(rank_z * rank_out)
+    z_pick = slim // rank_out == np.arange(rank_z)[:, None]
+    out_pick = slim % rank_out == np.arange(rank_out)[:, None]
+    return [pick.astype(np.float32) for pick in (x_pick, in_pick, z_pick, out_pick)]
+
+
+def spread(values, pick, dim):
+    return lax.dot_general(
+        values, pick, (((dim,), (0,)), ((), ())), precision=lax.Precision.HIGHEST,
+        preferred_element_type=F32,
+    )
+
+
+def fused_kernel(
+    width_gx, width_col, field_ref, core_ref, in_ref, out_factor_ref, x_ref, z_ref, reach_ref,
+    x_pick_ref, in_pick_ref, z_pick_ref, out_pick_ref, y_table_ref, z_table_ref, fore_ref, back_ref,
+    out_ref, field, y_high, y_low, spec, arrived, cores, factor, factors, rank_ref, high_ref,
+    low_ref, plane_ref, result_ref, field_sems, sends, recvs, core_sends, core_recvs, factor_sends,
+    factor_recvs, back_sends, back_recvs, own,
+):
+    count = width_gx * width_col
+    my_gx, my_col = lax.axis_index("gx"), lax.axis_index("col")
+    me = my_gx * width_col + my_col
+    channels, planes, _, grid_z = field.shape
+    groups, modes_y, group, lanes = spec.shape
+    modes_x, modes_z = x_ref.shape[1], z_ref.shape[1]
+    barrier = pltpu.get_barrier_semaphore()
+
+    def fetch(channel):
+        return pltpu.make_async_copy(
+            field_ref.at[channel], field.at[channel], field_sems.at[channel]
+        )
+
+    def begin(channel, carry):
+        fetch(channel).start()
+        return carry
+
+    lax.fori_loop(0, channels, begin, 0)
+
+    def place(peer):
+        return peer // width_col, lax.rem(peer, width_col)
+
+    def greet(step, carry):
+        peer = lax.rem(me + step, count)
+        pl.semaphore_signal(barrier, inc=1, device_id=place(peer), device_id_type=MESH)
+        return carry
+
+    lax.fori_loop(1, count, greet, 0)
+
+    def remote(source, target, send_sem, recv_sem, device):
+        return pltpu.make_async_remote_copy(
+            src_ref=source, dst_ref=target, send_sem=send_sem, recv_sem=recv_sem,
+            device_id=device, device_id_type=MESH,
+        )
+
+    in_wide = spread(in_ref[...], in_pick_ref[...], 1)
+    factor[:channels] = in_wide[:, :lanes]
+    factor[channels : 2 * channels] = in_wide[:, lanes:]
+    factor[2 * channels :] = spread(out_factor_ref[...], out_pick_ref[...], 1)
+
+    def spectrum_copy(part, peer, writer, device):
+        return remote(
+            spec.at[part, peer], arrived.at[part, writer], sends.at[part, peer],
+            recvs.at[part, writer], device,
+        )
+
+    def core_copy(peer, writer, device):
+        return remote(
+            core_ref.at[peer], cores.at[writer], core_sends.at[peer], core_recvs.at[writer], device
+        )
+
+    def factor_copy(peer, writer, device):
+        return remote(
+            factor, factors.at[writer], factor_sends.at[peer], factor_recvs.at[writer], device
+        )
+
+    half = 2 * modes_y
+    pair = 2
+    for part in range(groups):
+
+        def transform(step, carry, part=part):
+            for offset in range(pair):
+                local = step * pair + offset
+                channel = part * group + local
+                fetch(channel).wait()
+                parts = []
+                for plane in range(planes):
+                    both = dot(y_table_ref[...], field[channel, plane])
+                    y_values = both[:half] + both[half:]
+                    parts += [y_values[:modes_y], y_values[modes_y:]]
+                high, low = split(jnp.concatenate(parts, 1))
+                rows = pl.ds(pl.multiple_of(local * modes_y, modes_y), modes_y)
+                y_high[rows] = high
+                y_low[rows] = low
+            return carry
+
+        lax.fori_loop(0, group // pair, transform, 0)
+        both = dot(y_high[...], z_table_ref[...])
+        value = both[:, :lanes] + both[:, lanes:] + dot(y_low[...], z_table_ref[:, :lanes])
+        spec[part] = jnp.swapaxes(value.reshape(group, modes_y, lanes), 0, 1)
+        if part == 0:
+            pl.semaphore_wait(barrier, count - 1)
+            for step in range(1, width_col):
+                peer = lax.rem(my_col + step, width_col)
+                factor_copy(peer, my_col, (my_gx, peer)).start()
+                core_copy(peer, my_col, (my_gx, peer)).start()
+            pltpu.make_async_copy(core_ref.at[my_col], cores.at[my_col], own.at[0]).start()
+            pltpu.make_async_copy(factor, factors.at[my_col], own.at[1]).start()
+        pltpu.make_async_copy(spec.at[part, me], arrived.at[part, me], own.at[3 + part]).start()
+
+        def send(step, carry, part=part):
+            peer = lax.rem(me + step, count)
+            spectrum_copy(part, peer, me, place(peer)).start()
+            return carry
+
+        lax.fori_loop(1, count, send, 0)
+
+    x_wide = spread(x_ref[...], x_pick_ref[...], 0)
+    x_rows = jnp.concatenate([x_wide] * 4, 0)
+    z_rows = spread(z_ref[...], z_pick_ref[...], 0)
+    spot = lax.broadcasted_iota(jnp.int32, reach_ref.shape, 1)
+    reach = jnp.where(spot == me, reach_ref[...].astype(F32), 0.0)
+    reach = jnp.sum(reach, axis=1, keepdims=True)
+    slot = lax.broadcasted_iota(jnp.int32, (modes_x, x_rows.shape[1]), 0)
+    slot = jnp.where(slot < modes_x // 2, slot, modes_x - slot).astype(F32)
+    slot = jnp.concatenate([slot] * 4, 0)
+
+    for step in range(1, width_col):
+        source = lax.rem(my_col + step, width_col)
+        factor_copy(source, source, (my_gx, my_col)).wait_recv()
+        core_copy(source, source, (my_gx, my_col)).wait_recv()
+    pltpu.make_async_copy(core_ref.at[my_col], cores.at[my_col], own.at[0]).wait()
+    pltpu.make_async_copy(factor, factors.at[my_col], own.at[1]).wait()
+
+    lead = lanes // modes_z
+    both_modes = 2 * modes_x
+    ranks = x_rows.shape[1]
+    core_rows = ranks // width_col
+
+    def stacked_rows(ref, first, rows):
+        return ref[:, first : first + rows, :].reshape(width_col * rows, lanes)
+
+    in_rows = jnp.concatenate(
+        [stacked_rows(factors, 0, channels), stacked_rows(factors, channels, channels)], 1
+    )
+    out_rows = stacked_rows(factors, 2 * channels, channels)
+    in_high, in_low = split(in_rows)
+    in_stack = jnp.concatenate([in_high, in_low, in_high], 0)
+    core = jnp.concatenate(
+        [stacked_rows(cores, 0, core_rows), stacked_rows(cores, core_rows, core_rows)], 0
+    )
+    core_high, core_low = split(core)
+    core_both = jnp.concatenate([core_high, core_low], 1)
+    out_high, out_low = split(out_rows)
+    out_stack = jnp.concatenate([out_high, out_low], 0)
+
+    for part in range(groups):
+        pltpu.make_async_copy(spec.at[part, me], arrived.at[part, me], own.at[3 + part]).wait()
+
+        def receive(step, carry, part=part):
+            source = lax.rem(me + count - step, count)
+            spectrum_copy(part, source, source, (my_gx, my_col)).wait_recv()
+            return carry
+
+        lax.fori_loop(1, count, receive, 0)
+
+    for slab in range(width_gx):
+        blocks = [
+            arrived[part, slab * width_col + source]
+            for source in range(width_col)
+            for part in range(groups)
+        ]
+        block = jnp.concatenate(blocks, 0)
+        high = block.astype(BF16).astype(F32)
+        stacked = jnp.concatenate([high, high, block - high], 0)
+        value = dot(stacked.T.astype(BF16), in_stack)
+        rank_ref[:, slab * lead : (slab + 1) * lead, :] = value.reshape(modes_z, lead, ranks)
+    for l in range(modes_z):
+        high, low = split(rank_ref[l])
+        value = dot(fore_ref[...], jnp.concatenate([high, low, high], 0))
+        value = value * jnp.where(slot < reach[l : l + 1], x_rows, 0.0)
+        value = jnp.concatenate([value[:both_modes], value[both_modes:]], 1)
+        rows = slice(l * both_modes, (l + 1) * both_modes)
+        high_ref[rows], low_ref[rows] = split(value)
+    both = dot(high_ref[...], core_both)
+    mixed = both[:, :lanes] + both[:, lanes:] + dot(low_ref[...], core_high)
+    for l in range(modes_z):
+        value = mixed[l * both_modes : (l + 1) * both_modes] * z_rows[l : l + 1]
+        high, low = split(value)
+        value = dot(back_ref[...], jnp.concatenate([high, low, high], 0))
+        plane_ref[:, l] = value.reshape(width_gx, lead, lanes)
+
+    def back_copy(peer, writer, device):
+        return remote(
+            result_ref.at[peer], out_ref.at[writer], back_sends.at[peer], back_recvs.at[writer],
+            device,
+        )
+
+    rows_out = out_high.shape[0]
+    last = (((1,), (1,)), ((), ()))
+
+    def send_slab(slab):
+        for step in range(width_col):
+            peer_col = lax.rem(my_col + step, width_col)
+            peer = slab * width_col + peer_col
+
+            @pl.when(peer != me)
+            def _(peer=peer, peer_col=peer_col):
+                back_copy(peer, me, (slab, peer_col)).start()
+
+    for step in range(width_gx):
+        slab = lax.rem(my_gx + step, width_gx)
+        high, low = split(plane_ref[slab].reshape(lanes, lanes))
+        both = lax.dot_general(out_stack, high, last, preferred_element_type=F32)
+        value = both[:rows_out] + both[rows_out:]
+        value = value + lax.dot_general(out_high, low, last, preferred_element_type=F32)
+        result_ref[pl.ds(slab * width_col, width_col)] = value.reshape(width_col, channels, lanes)
+        if step > 0:
+            send_slab(lax.rem(my_gx + step - 1, width_gx))
+    send_slab(lax.rem(my_gx + width_gx - 1, width_gx))
+    keep = pltpu.make_async_copy(result_ref.at[me], out_ref.at[me], own.at[2])
+    keep.start()
+
+    def finish_sends(step, carry):
+        peer = lax.rem(me + step, count)
+        for part in range(groups):
+            spectrum_copy(part, peer, me, place(peer)).wait_send()
+        return carry
+
+    lax.fori_loop(1, count, finish_sends, 0)
+    for step in range(1, width_col):
+        peer = lax.rem(my_col + step, width_col)
+        factor_copy(peer, my_col, (my_gx, peer)).wait_send()
+        core_copy(peer, my_col, (my_gx, peer)).wait_send()
+
+    def finish(step, carry):
+        peer = lax.rem(me + step, count)
+        back_copy(peer, me, place(peer)).wait_send()
+        source = lax.rem(me + count - step, count)
+        back_copy(source, source, (my_gx, my_col)).wait_recv()
+        return carry
+
+    lax.fori_loop(1, count, finish, 0)
+    keep.wait()
+
+
+def fused(
+    grid_field, core, in_factor, out_factor, x_factor, z_factor, kx_reach, width_gx, width_col,
+    rank_dev,
+):
+    channels, planes, grid_y, grid_z = grid_field.shape
+    modes_x, rank_x = x_factor.shape
+    modes_z, rank_z = z_factor.shape
+    modes_y, rank_out = kx_reach.shape[0], out_factor.shape[1]
+    y_table, z_table = forward_tables(grid_y, grid_z, modes_y, modes_z, planes)
+    fore, back = x_tables(planes * width_gx, modes_x)
+    picks = selectors(width_col, rank_x, rank_dev, rank_z, rank_out)
+    count = width_gx * width_col
+    lanes, wide = planes * 2 * modes_z, planes * 2 * grid_z
+    ranks = width_col * rank_x * rank_dev
+    group = 8
+    groups = channels // group
+    dma = pltpu.SemaphoreType.DMA
+    tables = [jnp.asarray(t) for t in picks + [y_table, z_table, fore, back]]
+    return pl.pallas_call(
+        functools.partial(fused_kernel, width_gx, width_col),
+        out_shape=jax.ShapeDtypeStruct((count, channels, lanes), F32),
+        in_specs=[pl.BlockSpec(memory_space=pl.ANY)] + [VMEM] * (6 + len(tables)),
+        out_specs=VMEM,
+        scratch_shapes=[
+            pltpu.VMEM(grid_field.shape, BF16),
+            pltpu.VMEM((group * modes_y, wide), BF16),
+            pltpu.VMEM((group * modes_y, wide), BF16),
+            pltpu.VMEM((groups, modes_y, group, lanes), F32),
+            pltpu.VMEM((groups, count, group, lanes), F32),
+            pltpu.VMEM(core.shape, F32),
+            pltpu.VMEM((3 * channels, lanes), F32),
+            pltpu.VMEM((width_col, 3 * channels, lanes), F32),
+            pltpu.VMEM((modes_z, 2 * planes * width_gx, ranks), F32),
+            pltpu.VMEM((modes_z * 2 * modes_x, 2 * ranks), BF16),
+            pltpu.VMEM((modes_z * 2 * modes_x, 2 * ranks), BF16),
+            pltpu.VMEM((width_gx, modes_z, lanes // modes_z, lanes), F32),
+            pltpu.VMEM((count, channels, lanes), F32),
+            dma((channels,)),
+            dma((groups, count)),
+            dma((groups, count)),
+            dma((width_col,)),
+            dma((width_col,)),
+            dma((width_col,)),
+            dma((width_col,)),
+            dma((count,)),
+            dma((count,)),
+            dma((3 + groups,)),
+        ],
+        compiler_params=pltpu.CompilerParams(
+            collective_id=0, has_side_effects=True, vmem_limit_bytes=48 * 2**20
+        ),
+    )(grid_field, core, in_factor, out_factor, x_factor.T, z_factor.T, kx_reach.T, *tables)
+
+
+def inverse_kernel(spec_ref, y_ref, z_high_ref, z_low_ref, out_ref, high_ref, low_ref):
+    step = pl.program_id(0)
+    modes_y, channels, lanes = spec_ref.shape
+    block, planes, grid_z = out_ref.shape[0], out_ref.shape[1], out_ref.shape[3]
+    group = 8
+    for part in range(channels // group):
+
+        @pl.when(step * block == part * group)
+        def _(part=part):
+            values = spec_ref[:, part * group : (part + 1) * group]
+            values = jnp.swapaxes(values, 0, 1).reshape(-1, lanes)
+            high, low = split(values)
+            result = dot(high, z_high_ref[...]) + dot(high, z_low_ref[...])
+            result = result + dot(low, z_high_ref[...])
+            rows = slice(part * group * modes_y, (part + 1) * group * modes_y)
+            high_ref[rows], low_ref[rows] = split(result)
+
+    def tall(values, plane):
+        at = 2 * plane * grid_z
+        return [values[:, at : at + grid_z], values[:, at + grid_z : at + 2 * grid_z]]
+
+    for local in range(block):
+        first = (step * block + local) * modes_y
+        rows = pl.ds(pl.multiple_of(first, modes_y), modes_y)
+        high, low = high_ref[rows], low_ref[rows]
+        stacks = []
+        for plane in range(planes):
+            high_part = tall(high, plane)
+            stacks.append(jnp.concatenate(high_part + tall(low, plane) + high_part, 0))
+        for plane in range(0, planes, 2):
+            value = dot(y_ref[...], jnp.concatenate(stacks[plane : plane + 2], 1)).astype(BF16)
+            out_ref[local, plane] = value[:, :grid_z]
+            out_ref[local, plane + 1] = value[:, grid_z:]
+
+
+def inverse(returned, planes, grid_y, grid_z, modes_z):
+    modes_y, channels, _ = returned.shape
+    y_table, z_high, z_low = inverse_tables(grid_y, grid_z, modes_y, modes_z, planes)
+    wide = planes * 2 * grid_z
+    block = 4
+    return pl.pallas_call(
+        inverse_kernel,
+        grid=(channels // block,),
+        in_specs=[
+            pl.BlockSpec(returned.shape, lambda i: (0, 0, 0)),
+            pl.BlockSpec(y_table.shape, lambda i: (0, 0)),
+            pl.BlockSpec(z_high.shape, lambda i: (0, 0)),
+            pl.BlockSpec(z_low.shape, lambda i: (0, 0)),
+        ],
+        out_specs=pl.BlockSpec((block, planes, grid_y, grid_z), lambda i: (i, 0, 0, 0)),
+        out_shape=jax.ShapeDtypeStruct((channels, planes, grid_y, grid_z), BF16),
+        scratch_shapes=[
+            pltpu.VMEM((channels * modes_y, wide), BF16),
+            pltpu.VMEM((channels * modes_y, wide), BF16),
+        ],
+    )(returned, jnp.asarray(y_table), jnp.asarray(z_high), jnp.asarray(z_low))
+
+
+def row_device(
+    grid_field, tucker_core, in_factor, out_factor, x_factor, y_factor, z_factor, kx_reach
+):
+    _, planes, grid_y, grid_z = grid_field.shape
+    width_gx, width_col = lax.axis_size("gx"), lax.axis_size("col")
+    rank_out = out_factor.shape[1]
+    rank_dev, rank_x, rank_z = tucker_core.shape[1], x_factor.shape[1], z_factor.shape[1]
+    y_rows = lax.dynamic_slice_in_dim(y_factor, lax.axis_index("gx") * width_col, width_col)
+    core = jnp.einsum("prsabe,db->dpares", tucker_core, y_rows, precision=lax.Precision.HIGHEST)
+    core = core.reshape(width_col, 2 * rank_x * rank_dev, rank_z * rank_out)
+    returned = fused(
+        grid_field, core, in_factor, out_factor, x_factor, z_factor, kx_reach, width_gx, width_col,
+        rank_dev,
+    )
+    return inverse(returned, planes, grid_y, grid_z, z_factor.shape[0])
+
+
+def per_device(
+    grid_field, tucker_core, in_factor, out_factor, x_factor, y_factor, z_factor, kx_reach
+):
+    planes, grid_z = grid_field.shape[1], grid_field.shape[3]
+    modes_y, modes_z = y_factor.shape[0], z_factor.shape[0]
+    devices = lax.axis_size("gx") * lax.axis_size("col")
+    ranks = in_factor.shape[1] * x_factor.shape[1]
+    row_each = (
+        devices == modes_y
+        and planes == 4
+        and grid_field.shape[0] % 8 == 0
+        and grid_z == 128
+        and planes * 2 * modes_z == 128
+        and ranks == 256
+        and out_factor.shape[1] * z_factor.shape[1] == 128
+    )
+    device = row_device if row_each else plain_device
+    return device(
+        grid_field, tucker_core, in_factor, out_factor, x_factor, y_factor, z_factor, kx_reach
+    )
+
+
 def solution(mesh):
     return jax.shard_map(
         per_device,

time: 164 us -> 43.5 us (0.27)
  waiting for transfers between devices: 63.9 us -> 0 us
  matrix products: 46.9 us -> 2.63 us
  Pallas kernels: 0 us -> 32.8 us
  between operations: 13.6 us -> 0.25 us
  starting transfers between devices: 13.1 us -> 0 us
  other arithmetic: 10.8 us -> 0 us
  local copies, waits for them, and re-layouts: 15.6 us -> 7.48 us
    dot_general x12 -> x1, matrix products: 46.9 us -> 2.63 us  [row_device(): jnp.einsum('prsabe,db->dpares', tucker_core, y_rows, precision=lax.Precis...]
    psum x1 -> x0, waiting for transfers between devices: 36.5 us -> none  [per_device(): mixed_sum = lax.psum(jnp.stack([mixed_re, mixed_im]), 'col')]
    pallas_call x0 -> x2, Pallas kernels: none -> 32.8 us  [the longest x1 27.3 us: fused(): pl.pallas_call(functools.partial(fused_kernel, width_gx, width_col), out_...]
    all_to_all x2 -> x0, waiting for transfers between devices: 16.9 us -> none  [the longest x1 8.47 us: per_device(): lax.all_to_all(y_spectrum, 'gx', split_axis=3, concat_axis=2, tiled=True)]
    all_to_all x2 -> x0, starting transfers between devices: 12.8 us -> none  [the longest x1 7.29 us: per_device(): lax.all_to_all(y_spectrum, 'gx', split_axis=3, concat_axis=2, tiled=True)]
    reduce_scatter x1 -> x0, waiting for transfers between devices: 10.5 us -> none  [per_device(): lax.psum_scatter(partial_value, 'col', scatter_dimension=1, tiled=True)]
    unnamed x1 -> x0, other arithmetic: 4.65 us -> none
    unnamed x22 -> x32, local copies, waits for them, and re-layouts: 7.99 us -> 4.55 us
  transfers between devices with their start and end apart: 4 -> 0, of which waited for: 4 -> 0; matrix products, arithmetic and copies ran while one was open for 8% -> 0% of each run, Pallas kernels for 0% -> 0%
where the time goes in v2:
time: 43.5 us; the launch traced here: 43.2 us
  Pallas kernels  32.8 us (75%)
  local copies, waits for them, and re-layouts  7.48 us (17%)
  matrix products  2.63 us (6%)
    pallas_call x1, Pallas kernels, fused(): pl.pallas_call(functools.partial(fused_kernel, width_gx, width_col), out_...  27.3 us
    pallas_call x1, Pallas kernels, inverse(): pl.pallas_call(inverse_kernel, grid=(channels // block,), in_specs=[pl.Bl...  5.57 us
    unnamed x32, local copies, waits for them, and re-layouts  4.55 us
    dot_general x1, matrix products, row_device(): jnp.einsum('prsabe,db->dpares', tucker_core, y_rows, precision=lax.Precis...  2.63 us
    reshape x1, local copies, waits for them, and re-layouts, row_device(): core = core.reshape(width_col, 2 * rank_x * rank_dev, rank_z * rank_out)  1.69 us
    transpose x1, local copies, waits for them, and re-layouts, row_device(): jnp.einsum('prsabe,db->dpares', tucker_core, y_rows, precision=lax.Precis...  1.24 us

profile of v2, /device:TPU:0, one launch (start us, length us, event | category | flops | bytes accessed | tf_op | source)
XLA Modules:
  0.0 43.2 jit_solution(1065160529758356822)
XLA Ops:
  0.0 0.0 copy-start
  0.0 1.6 %copy-done = f32[2,8,32,8,8,4]{2,5,4,3,1,0:T(4,128)S(1)} copy-done((f32[2,8,32,8,8,4]{2,5,4,3,1,0:T(4,128)S(1)}, f32[2,8,32,8,8,4]{2,5,4,3,1,0:T(4,128)}, u32[]{:S(2)}) %copy-start) | copy-done | bytes 524312
  1.6 2.6 %fusion.2 = f32[4,2,8,8,4,32]{5,0,4,2,3,1:T(4,128)S(1)} fusion(f32[2,8,32,8,8,4]{2,5,4,3,1,0:T(4,128)S(1)} %copy-done, f32[32,8]{0,1:T(8,128)} %param.24, s32[]{:T(128)S(6)} %select_n.3), kind=kOutput, calls=%fused_computation.2 | convolution fusion | flops 6291456 | bytes 787460 | tf_op jit(solution)/shard_map/prsabe,db->dpares/dot_general | solution.py:545
  4.2 0.0 copy-start.3
  4.2 0.0 copy-start.4
  4.3 0.0 copy-start.5
  4.3 0.0 copy-start.6
  4.3 0.0 copy-start.7
  4.3 0.0 copy-start.8
  4.3 0.0 copy-start.9
  4.3 0.0 copy-start.10
  4.3 0.0 copy-start.11
  4.3 0.0 copy-start.12
  4.4 0.0 copy-start.13
  4.4 0.0 copy-start.14
  4.4 0.0 copy-start.15
  4.4 1.2 %copy.22 = f32[4,2,8,8,4,32]{5,4,3,2,1,0:T(4,128)} copy(f32[4,2,8,8,4,32]{5,0,4,2,3,1:T(4,128)S(1)} %fusion.2) | data formatting | bytes 524288 | tf_op jit(solution)/shard_map/prsabe,db->dpares/transpose | solution.py:545
  5.6 1.7 %reshape.3.core_ref = f32[4,128,128]{2,1,0:T(8,128)S(1)} reshape(f32[4,2,8,8,4,32]{5,4,3,2,1,0:T(4,128)} %copy.22) | data formatting | bytes 524288 | tf_op jit(solution)/shard_map/reshape | solution.py:546
  7.3 0.0 copy-done.3
  7.3 0.0 copy-done.4
  7.3 0.0 copy-done.5
  7.4 0.0 copy-done.6
  7.4 0.0 copy-done.7
  7.4 0.0 copy-done.8
  7.4 0.0 copy-done.9
  7.4 0.0 copy-done.10
  7.4 0.0 copy-done.11
  7.4 0.0 copy-done.12
  7.4 0.0 copy-done.13
  7.4 0.0 copy-done.14
  7.4 0.0 copy-done.15
  7.5 0.0 copy-start.1
  7.5 2.2 %copy-done.1 = bf16[16,4,256,128]{3,2,1,0:T(8,128)(2,1)S(1)} copy-done((bf16[16,4,256,128]{3,2,1,0:T(8,128)(2,1)S(1)}, bf16[16,4,256,128]{3,2,1,0:T(8,128)(2,1)}, u32[]{:S(2)}) %copy-start.1) | copy-done | bytes 4194328
  9.6 27.3 %shard_map.181.spec_ref = f32[32,16,128]{2,1,0:T(8,128)S(1)} custom-call(bf16[16,4,256,128]{3,2,1,0:T(8,128)(2,1)S(1)} %copy-done.1, f32[4,128,128]{2,1,0:T(8,128)S(1)} %reshape.3.core_ref, f32[16,32]{1,0:T(8,128)S(1)} %copy-done.9, f32[16,32]{1,0:T(8,128)S(1)} %copy-done.10, f32[8,32]{1,0:T(8,128)S(1)} %bitcast.12, f32[4,16]{1,0:T(4,128)S(1)} %bitcast.13, ...), custom_call_target="tpu_custom_call" | custom-call | tf_op jit(solution)/shard_map/pallas_call | solution.py:443
  36.9 0.0 copy-start.2
  36.9 0.7 %copy-done.2 = f32[32,16,128]{2,1,0:T(8,128)} copy-done((f32[32,16,128]{2,1,0:T(8,128)}, f32[32,16,128]{2,1,0:T(8,128)S(1)}, u32[]{:S(2)}) %copy-start.2) | copy-done | bytes 262168
  37.6 5.6 %shard_map.182 = bf16[16,4,256,128]{3,2,1,0:T(8,128)(2,1)} custom-call(f32[32,16,128]{2,1,0:T(8,128)} %copy-done.2, bf16[256,192]{1,0:T(8,128)(2,1)} %constant.42.clone.y_ref, bf16[128,1024]{1,0:T(8,128)(2,1)} %constant.43.clone.z_high_ref, bf16[128,1024]{1,0:T(8,128)(2,1)} %constant.44.clone.z_low_ref), custom_call_target="tpu_custom_call" | custom-call | tf_op jit(solution)/shard_map/pallas_call | solution.py:519
Async XLA Ops:
  0.0 1.6 %copy-start = (f32[2,8,32,8,8,4]{2,5,4,3,1,0:T(4,128)S(1)}, f32[2,8,32,8,8,4]{2,5,4,3,1,0:T(4,128)}, u32[]{:S(2)}) copy-start(f32[2,8,32,8,8,4]{2,5,4,3,1,0:T(4,128)} %param.20) | copy-start | bytes 1572868
  4.2 3.1 %copy-start.3 = (bf16[1024,256]{1,0:T(8,128)(2,1)S(1)}, bf16[1024,256]{1,0:T(8,128)(2,1)}, u32[]{:S(2)}) copy-start(bf16[1024,256]{1,0:T(8,128)(2,1)} %constant.39.clone.z_table_ref) | copy-start | bytes 1572868
  4.2 3.1 %copy-start.4 = (bf16[128,192]{1,0:T(8,128)(2,1)S(1)}, bf16[128,192]{1,0:T(8,128)(2,1)}, u32[]{:S(2)}) copy-start(bf16[128,192]{1,0:T(8,128)(2,1)} %constant.40.clone.fore_ref) | copy-start | bytes 147460
  4.3 3.1 %copy-start.5 = (bf16[128,256]{1,0:T(8,128)(2,1)S(1)}, bf16[128,256]{1,0:T(8,128)(2,1)}, u32[]{:S(2)}) copy-start(bf16[128,256]{1,0:T(8,128)(2,1)} %constant.38.clone.y_table_ref) | copy-start | bytes 196612
  4.3 3.1 %copy-start.6 = (bf16[64,192]{1,0:T(8,128)(2,1)S(1)}, bf16[64,192]{1,0:T(8,128)(2,1)}, u32[]{:S(2)}) copy-start(bf16[64,192]{1,0:T(8,128)(2,1)} %constant.41.clone.back_ref) | copy-start | bytes 73732
  4.3 3.1 %copy-start.7 = (f32[32,256]{1,0:T(8,128)S(1)}, f32[32,256]{1,0:T(8,128)}, u32[]{:S(2)}) copy-start(f32[32,256]{1,0:T(8,128)} %constant.35.clone.in_pick_ref) | copy-start | bytes 98308
  4.3 3.1 %copy-start.8 = (f32[32,128]{1,0:T(8,128)S(1)}, f32[32,128]{1,0:T(8,128)}, u32[]{:S(2)}) copy-start(f32[32,128]{1,0:T(8,128)} %constant.37.clone.out_pick_ref) | copy-start | bytes 49156
  4.3 3.1 %copy-start.9 = (f32[16,32]{1,0:T(8,128)S(1)}, f32[16,32]{1,0:T(8,128)}, u32[]{:S(2)}) copy-start(f32[16,32]{1,0:T(8,128)} %in_ref.1) | copy-start | bytes 6148
  4.3 3.1 %copy-start.10 = (f32[16,32]{1,0:T(8,128)S(1)}, f32[16,32]{1,0:T(8,128)}, u32[]{:S(2)}) copy-start(f32[16,32]{1,0:T(8,128)} %out_factor_ref.1) | copy-start | bytes 6148
  4.3 3.1 %copy-start.11 = (s32[32,16]{0,1:T(8,128)S(1)}, s32[32,16]{0,1:T(8,128)}, u32[]{:S(2)}) copy-start(s32[32,16]{0,1:T(8,128)} %param.26) | copy-start | bytes 6148
  4.3 3.1 %copy-start.12 = (f32[8,256]{1,0:T(8,128)S(1)}, f32[8,256]{1,0:T(8,128)}, u32[]{:S(2)}) copy-start(f32[8,256]{1,0:T(8,128)} %constant.34.clone.x_pick_ref) | copy-start | bytes 24580
  4.4 3.1 %copy-start.13 = (f32[32,8]{0,1:T(8,128)S(1)}, f32[32,8]{0,1:T(8,128)}, u32[]{:S(2)}) copy-start(f32[32,8]{0,1:T(8,128)} %param.23) | copy-start | bytes 3076
  4.4 3.1 %copy-start.14 = (f32[16,4]{0,1:T(4,128)S(1)}, f32[16,4]{0,1:T(4,128)}, u32[]{:S(2)}) copy-start(f32[16,4]{0,1:T(4,128)} %param.25) | copy-start | bytes 772
  4.4 3.1 %copy-start.15 = (f32[4,128]{1,0:T(4,128)S(1)}, f32[4,128]{1,0:T(4,128)}, u32[]{:S(2)}) copy-start(f32[4,128]{1,0:T(4,128)} %constant.36.clone.z_pick_ref) | copy-start | bytes 6148
  7.5 2.2 %copy-start.1 = (bf16[16,4,256,128]{3,2,1,0:T(8,128)(2,1)S(1)}, bf16[16,4,256,128]{3,2,1,0:T(8,128)(2,1)}, u32[]{:S(2)}) copy-start(bf16[16,4,256,128]{3,2,1,0:T(8,128)(2,1)} %field_ref.1) | copy-start | bytes 12582916
  36.9 0.7 %copy-start.2 = (f32[32,16,128]{2,1,0:T(8,128)}, f32[32,16,128]{2,1,0:T(8,128)S(1)}, u32[]{:S(2)}) copy-start(f32[32,16,128]{2,1,0:T(8,128)S(1)} %shard_map.181.spec_ref) | copy-start | bytes 786436

commit v3 on v2

--- a/solution.py
+++ b/solution.py
@@ -443,7 +443,7 @@
     return pl.pallas_call(
         functools.partial(fused_kernel, width_gx, width_col),
         out_shape=jax.ShapeDtypeStruct((count, channels, lanes), F32),
-        in_specs=[pl.BlockSpec(memory_space=pl.ANY)] + [VMEM] * (6 + len(tables)),
+        in_specs=[pl.BlockSpec(memory_space=pltpu.HBM)] + [VMEM] * (6 + len(tables)),
         out_specs=VMEM,
         scratch_shapes=[
             pltpu.VMEM(grid_field.shape, BF16),

time: 43.5 us -> 43.5 us (level)
  no operation moved by 1% of the time
where the time goes in v3:
time: 43.5 us; the launch traced here: 43.2 us
  Pallas kernels  32.8 us (75%)
  local copies, waits for them, and re-layouts  7.48 us (17%)
  matrix products  2.63 us (6%)
    pallas_call x1, Pallas kernels, fused(): pl.pallas_call(functools.partial(fused_kernel, width_gx, width_col), out_...  27.3 us
    pallas_call x1, Pallas kernels, inverse(): pl.pallas_call(inverse_kernel, grid=(channels // block,), in_specs=[pl.Bl...  5.57 us
    unnamed x32, local copies, waits for them, and re-layouts  4.55 us
    dot_general x1, matrix products, row_device(): jnp.einsum('prsabe,db->dpares', tucker_core, y_rows, precision=lax.Precis...  2.63 us
    reshape x1, local copies, waits for them, and re-layouts, row_device(): core = core.reshape(width_col, 2 * rank_x * rank_dev, rank_z * rank_out)  1.69 us
    transpose x1, local copies, waits for them, and re-layouts, row_device(): jnp.einsum('prsabe,db->dpares', tucker_core, y_rows, precision=lax.Precis...  1.24 us

profile of v3, /device:TPU:0, one launch (start us, length us, event | category | flops | bytes accessed | tf_op | source)
XLA Modules:
  0.0 43.2 jit_solution(1065160529758356822)
XLA Ops:
  0.0 0.0 copy-start
  0.0 1.6 %copy-done = f32[2,8,32,8,8,4]{2,5,4,3,1,0:T(4,128)S(1)} copy-done((f32[2,8,32,8,8,4]{2,5,4,3,1,0:T(4,128)S(1)}, f32[2,8,32,8,8,4]{2,5,4,3,1,0:T(4,128)}, u32[]{:S(2)}) %copy-start) | copy-done | bytes 524312
  1.6 2.6 %fusion.2 = f32[4,2,8,8,4,32]{5,0,4,2,3,1:T(4,128)S(1)} fusion(f32[2,8,32,8,8,4]{2,5,4,3,1,0:T(4,128)S(1)} %copy-done, f32[32,8]{0,1:T(8,128)} %param.24, s32[]{:T(128)S(6)} %select_n.3), kind=kOutput, calls=%fused_computation.2 | convolution fusion | flops 6291456 | bytes 787460 | tf_op jit(solution)/shard_map/prsabe,db->dpares/dot_general | solution.py:545
  4.2 0.0 copy-start.3
  4.2 0.0 copy-start.4
  4.3 0.0 copy-start.5
  4.3 0.0 copy-start.6
  4.3 0.0 copy-start.7
  4.3 0.0 copy-start.8
  4.3 0.0 copy-start.9
  4.3 0.0 copy-start.10
  4.3 0.0 copy-start.11
  4.3 0.0 copy-start.12
  4.4 0.0 copy-start.13
  4.4 0.0 copy-start.14
  4.4 0.0 copy-start.15
  4.4 1.2 %copy.22 = f32[4,2,8,8,4,32]{5,4,3,2,1,0:T(4,128)} copy(f32[4,2,8,8,4,32]{5,0,4,2,3,1:T(4,128)S(1)} %fusion.2) | data formatting | bytes 524288 | tf_op jit(solution)/shard_map/prsabe,db->dpares/transpose | solution.py:545
  5.6 1.7 %reshape.3.core_ref = f32[4,128,128]{2,1,0:T(8,128)S(1)} reshape(f32[4,2,8,8,4,32]{5,4,3,2,1,0:T(4,128)} %copy.22) | data formatting | bytes 524288 | tf_op jit(solution)/shard_map/reshape | solution.py:546
  7.3 0.0 copy-done.3
  7.3 0.0 copy-done.4
  7.3 0.0 copy-done.5
  7.4 0.0 copy-done.6
  7.4 0.0 copy-done.7
  7.4 0.0 copy-done.8
  7.4 0.0 copy-done.9
  7.4 0.0 copy-done.10
  7.4 0.0 copy-done.11
  7.4 0.0 copy-done.12
  7.4 0.0 copy-done.13
  7.4 0.0 copy-done.14
  7.4 0.0 copy-done.15
  7.5 0.0 copy-start.1
  7.5 2.2 %copy-done.1 = bf16[16,4,256,128]{3,2,1,0:T(8,128)(2,1)S(1)} copy-done((bf16[16,4,256,128]{3,2,1,0:T(8,128)(2,1)S(1)}, bf16[16,4,256,128]{3,2,1,0:T(8,128)(2,1)}, u32[]{:S(2)}) %copy-start.1) | copy-done | bytes 4194328
  9.6 27.3 %shard_map.181.spec_ref = f32[32,16,128]{2,1,0:T(8,128)S(1)} custom-call(bf16[16,4,256,128]{3,2,1,0:T(8,128)(2,1)S(1)} %copy-done.1, f32[4,128,128]{2,1,0:T(8,128)S(1)} %reshape.3.core_ref, f32[16,32]{1,0:T(8,128)S(1)} %copy-done.9, f32[16,32]{1,0:T(8,128)S(1)} %copy-done.10, f32[8,32]{1,0:T(8,128)S(1)} %bitcast.12, f32[4,16]{1,0:T(4,128)S(1)} %bitcast.13, ...), custom_call_target="tpu_custom_call" | custom-call | tf_op jit(solution)/shard_map/pallas_call | solution.py:443
  36.9 0.0 copy-start.2
  36.9 0.7 %copy-done.2 = f32[32,16,128]{2,1,0:T(8,128)} copy-done((f32[32,16,128]{2,1,0:T(8,128)}, f32[32,16,128]{2,1,0:T(8,128)S(1)}, u32[]{:S(2)}) %copy-start.2) | copy-done | bytes 262168
  37.6 5.6 %shard_map.182 = bf16[16,4,256,128]{3,2,1,0:T(8,128)(2,1)} custom-call(f32[32,16,128]{2,1,0:T(8,128)} %copy-done.2, bf16[256,192]{1,0:T(8,128)(2,1)} %constant.42.clone.y_ref, bf16[128,1024]{1,0:T(8,128)(2,1)} %constant.43.clone.z_high_ref, bf16[128,1024]{1,0:T(8,128)(2,1)} %constant.44.clone.z_low_ref), custom_call_target="tpu_custom_call" | custom-call | tf_op jit(solution)/shard_map/pallas_call | solution.py:519
Async XLA Ops:
  0.0 1.6 %copy-start = (f32[2,8,32,8,8,4]{2,5,4,3,1,0:T(4,128)S(1)}, f32[2,8,32,8,8,4]{2,5,4,3,1,0:T(4,128)}, u32[]{:S(2)}) copy-start(f32[2,8,32,8,8,4]{2,5,4,3,1,0:T(4,128)} %param.20) | copy-start | bytes 1572868
  4.2 3.1 %copy-start.3 = (bf16[1024,256]{1,0:T(8,128)(2,1)S(1)}, bf16[1024,256]{1,0:T(8,128)(2,1)}, u32[]{:S(2)}) copy-start(bf16[1024,256]{1,0:T(8,128)(2,1)} %constant.39.clone.z_table_ref) | copy-start | bytes 1572868
  4.2 3.1 %copy-start.4 = (bf16[128,192]{1,0:T(8,128)(2,1)S(1)}, bf16[128,192]{1,0:T(8,128)(2,1)}, u32[]{:S(2)}) copy-start(bf16[128,192]{1,0:T(8,128)(2,1)} %constant.40.clone.fore_ref) | copy-start | bytes 147460
  4.3 3.1 %copy-start.5 = (bf16[128,256]{1,0:T(8,128)(2,1)S(1)}, bf16[128,256]{1,0:T(8,128)(2,1)}, u32[]{:S(2)}) copy-start(bf16[128,256]{1,0:T(8,128)(2,1)} %constant.38.clone.y_table_ref) | copy-start | bytes 196612
  4.3 3.1 %copy-start.6 = (bf16[64,192]{1,0:T(8,128)(2,1)S(1)}, bf16[64,192]{1,0:T(8,128)(2,1)}, u32[]{:S(2)}) copy-start(bf16[64,192]{1,0:T(8,128)(2,1)} %constant.41.clone.back_ref) | copy-start | bytes 73732
  4.3 3.1 %copy-start.7 = (f32[32,256]{1,0:T(8,128)S(1)}, f32[32,256]{1,0:T(8,128)}, u32[]{:S(2)}) copy-start(f32[32,256]{1,0:T(8,128)} %constant.35.clone.in_pick_ref) | copy-start | bytes 98308
  4.3 3.1 %copy-start.8 = (f32[32,128]{1,0:T(8,128)S(1)}, f32[32,128]{1,0:T(8,128)}, u32[]{:S(2)}) copy-start(f32[32,128]{1,0:T(8,128)} %constant.37.clone.out_pick_ref) | copy-start | bytes 49156
  4.3 3.1 %copy-start.9 = (f32[16,32]{1,0:T(8,128)S(1)}, f32[16,32]{1,0:T(8,128)}, u32[]{:S(2)}) copy-start(f32[16,32]{1,0:T(8,128)} %in_ref.1) | copy-start | bytes 6148
  4.3 3.1 %copy-start.10 = (f32[16,32]{1,0:T(8,128)S(1)}, f32[16,32]{1,0:T(8,128)}, u32[]{:S(2)}) copy-start(f32[16,32]{1,0:T(8,128)} %out_factor_ref.1) | copy-start | bytes 6148
  4.3 3.1 %copy-start.11 = (s32[32,16]{0,1:T(8,128)S(1)}, s32[32,16]{0,1:T(8,128)}, u32[]{:S(2)}) copy-start(s32[32,16]{0,1:T(8,128)} %param.26) | copy-start | bytes 6148
  4.3 3.1 %copy-start.12 = (f32[8,256]{1,0:T(8,128)S(1)}, f32[8,256]{1,0:T(8,128)}, u32[]{:S(2)}) copy-start(f32[8,256]{1,0:T(8,128)} %constant.34.clone.x_pick_ref) | copy-start | bytes 24580
  4.4 3.1 %copy-start.13 = (f32[32,8]{0,1:T(8,128)S(1)}, f32[32,8]{0,1:T(8,128)}, u32[]{:S(2)}) copy-start(f32[32,8]{0,1:T(8,128)} %param.23) | copy-start | bytes 3076
  4.4 3.1 %copy-start.14 = (f32[16,4]{0,1:T(4,128)S(1)}, f32[16,4]{0,1:T(4,128)}, u32[]{:S(2)}) copy-start(f32[16,4]{0,1:T(4,128)} %param.25) | copy-start | bytes 772
  4.4 3.1 %copy-start.15 = (f32[4,128]{1,0:T(4,128)S(1)}, f32[4,128]{1,0:T(4,128)}, u32[]{:S(2)}) copy-start(f32[4,128]{1,0:T(4,128)} %constant.36.clone.z_pick_ref) | copy-start | bytes 6148
  7.5 2.2 %copy-start.1 = (bf16[16,4,256,128]{3,2,1,0:T(8,128)(2,1)S(1)}, bf16[16,4,256,128]{3,2,1,0:T(8,128)(2,1)}, u32[]{:S(2)}) copy-start(bf16[16,4,256,128]{3,2,1,0:T(8,128)(2,1)} %field_ref.1) | copy-start | bytes 12582916
  36.9 0.7 %copy-start.2 = (f32[32,16,128]{2,1,0:T(8,128)}, f32[32,16,128]{2,1,0:T(8,128)S(1)}, u32[]{:S(2)}) copy-start(f32[32,16,128]{2,1,0:T(8,128)S(1)} %shard_map.181.spec_ref) | copy-start | bytes 786436
